TPU v7x, 128 devices: a whole 4x4x4 slice. The times are simulated.
128 devices in a mesh: grp: 4 (over x_lo, core), dev: 32 (over z, x_hi, y).
Axes of the slice: x: 4 (x_hi: 2, x_lo: 2; x = x_hi * 2 + x_lo), y: 4, z: 4, core: 2. Of those that a mesh axis runs over, the one named last changes fastest.
Arguments:
- student: bfloat16 [16384, 1024], P(('grp', 'dev')), may hold values from -0.19921875 to 0.19921875
- teacher: bfloat16 [16384, 1024], P(('grp', 'dev')), may hold values from -0.19921875 to 0.19921875
- labels: int32 [16384], P(('grp', 'dev')), may hold values from 0 to 999, as said below
Outputs:
- supcon_loss: float32 [], replicated
- relation_loss: float32 [], replicated
- feature_grad: float32 [16384, 1024], P(('grp', 'dev'))
Inputs may be any that keep to these rules, and one draw needn't show every extreme that they name: `labels`: each label from 875 upward belongs to exactly one view of the batch; every other view has a label below 875.
All inputs are finite; a program needn't handle non-finite values.
Results may differ from a plain program's by a relative error of at most 0.0003.
The roundings to bfloat16 on the way count: a program that leaves them out, or rounds other values in their place, can miss the bound.
Values may be sent and summed in bfloat16 or wider, within the bound.
A program may use at most 128 MiB of HBM per device.

v0:
```python
import functools
import math

import jax
import jax.numpy as jnp
from jax import lax
from jax.sharding import Mesh
from jax.sharding import PartitionSpec as P

GRP = ("grp_0", "grp_1")
DEV = ("dev_0", "dev_1", "dev_2")
GRP_DEV = ("grp_0", "grp_1", "dev_0", "dev_1", "dev_2")


temp_sup = 0.1
temp_student = 0.2
temp_teacher = 0.05
epsilon = 1e-06


def side_by_side(arrays, axis, dim, along):
    widths = [a.shape[along] for a in arrays]
    both = jnp.concatenate(arrays, axis=along)
    out = lax.all_gather(both, axis, axis=dim, tiled=True)
    return tuple(jnp.split(out, [sum(widths[:k]) for k in range(1, len(widths))], axis=along))


def sent_to_all(value, axis):
    copies = jnp.broadcast_to(value, (lax.axis_size(axis), *value.shape))
    return lax.all_to_all(copies, axis, split_axis=0, concat_axis=0, tiled=True)


def of_everyone(value, axis):
    return sent_to_all(value, axis).sum(axis=0)


def one_axis_at_a_time(value, axes):
    return functools.reduce(lax.psum, axes, value)


def joined_along(blocks, dim):
    blocks = jnp.moveaxis(blocks, 0, dim)
    lengths = blocks.shape
    return blocks.reshape(*lengths[:dim], lengths[dim] * lengths[dim + 1], *lengths[dim + 2 :])


def gathered_copies(value, axis, dim):
    blocks = sent_to_all(value, axis)
    return joined_along(blocks, dim)


def cut_along(value, dim, peers):
    before, after = (value.shape[:dim], value.shape[dim + 1 :])
    return jnp.moveaxis(value.reshape(*before, peers, -1, *after), dim, 0)


def summed_on_arrival(value, axis, dim):
    peers = lax.axis_size(axis)
    blocks = lax.all_to_all(cut_along(value, dim, peers), axis, 0, 0, tiled=True)
    return jnp.sum(blocks, axis=0)


def unit_rows(raw):
    values = raw.astype(jnp.float32)
    scaling = lax.rsqrt(jnp.sum(values * values, axis=1, keepdims=True) + epsilon)
    return (values * scaling, scaling)


def inner_rows(left, right):
    return lax.dot_general(
        left, right, (((1,), (1,)), ((), ())), preferred_element_type=jnp.float32
    )


def tile_terms(
    anchor_unit,
    anchor_teacher,
    anchor_label,
    anchor_place,
    key_unit,
    key_teacher,
    key_label,
    key_place,
):
    similar = inner_rows(anchor_unit, key_unit)
    teacher_sim = inner_rows(anchor_teacher, key_teacher)
    distinct = anchor_place[:, None] != key_place[None, :]
    positive = jnp.logical_and(anchor_label[:, None] == key_label[None, :], distinct).astype(
        jnp.float32
    )
    empty = jnp.zeros_like(similar)
    sup_exp = jnp.where(distinct, jnp.exp((similar - 1.0) / temp_sup), empty)
    rel_exp = jnp.where(distinct, jnp.exp((similar - 1.0) / temp_student), empty)
    teacher_exp = jnp.where(distinct, jnp.exp((teacher_sim - 1.0) / temp_teacher), empty)
    return (similar, positive, sup_exp, rel_exp, teacher_exp)


def tile_stats(terms):
    similar, positive, sup_exp, rel_exp, teacher_exp = terms
    return (
        jnp.sum(sup_exp, axis=1),
        jnp.sum(rel_exp, axis=1),
        jnp.sum(teacher_exp, axis=1),
        jnp.sum(teacher_exp * similar, axis=1),
        jnp.sum(positive * similar, axis=1),
        jnp.sum(positive, axis=1),
    )


def coefficient(terms, sup_total, rel_total, teacher_total, positives):
    similar, positive, sup_exp, rel_exp, teacher_exp = terms
    return (sup_exp / sup_total - positive / positives) / temp_sup + (
        rel_exp / rel_total - teacher_exp / teacher_total
    ) / temp_student


def row_losses(stats):
    sup_total, rel_total, teacher_total, teacher_mix, positive_sum, positive_count = stats
    positives = jnp.maximum(positive_count, 1.0)
    contrast = (1.0 - positive_sum / positives) / temp_sup + jnp.log(sup_total)
    relation = (1.0 - teacher_mix / teacher_total) / temp_student + jnp.log(rel_total)
    return (contrast, relation)


def coef_inputs(stats):
    return (stats[0], stats[1], stats[2], jnp.maximum(stats[5], 1.0))


def body(student, teacher, labels):
    row_count = student.shape[0]
    width = student.shape[1]
    groups = lax.axis_size(GRP)
    members = lax.axis_size(DEV)
    unit_student, scaling = unit_rows(student)
    unit_rounded = unit_student.astype(jnp.bfloat16)
    teacher_rounded = unit_rows(teacher)[0].astype(jnp.bfloat16)
    anchor_unit, anchor_teacher, anchor_label = (
        *side_by_side((unit_rounded, teacher_rounded), DEV, 0, 1),
        lax.all_gather(labels, DEV, axis=0, tiled=True),
    )
    key_unit, key_teacher, key_label = (
        *side_by_side((unit_rounded, teacher_rounded), GRP, 0, 1),
        lax.all_gather(labels, GRP, axis=0, tiled=True),
    )
    group_index = lax.axis_index(GRP)
    member_index = lax.axis_index(DEV)
    slab_rows = members * row_count
    key_count = groups * row_count
    view_count = row_count * groups * members
    anchor_place = group_index * slab_rows + jnp.arange(slab_rows, dtype=jnp.int32)
    key_place = (
        (jnp.arange(groups, dtype=jnp.int32)[:, None] * members + member_index) * row_count
        + jnp.arange(row_count, dtype=jnp.int32)[None, :]
    ).reshape(key_count)
    block_rows = math.gcd(slab_rows, 512)
    block_total = slab_rows // block_rows
    blocked = (
        anchor_unit.reshape(block_total, block_rows, width),
        anchor_teacher.reshape(block_total, block_rows, width),
        anchor_label.reshape(block_total, block_rows),
        anchor_place.reshape(block_total, block_rows),
    )

    def block_terms(operands):
        return tile_terms(
            operands[0],
            operands[1],
            operands[2],
            operands[3],
            key_unit,
            key_teacher,
            key_label,
            key_place,
        )

    def stats_block(operands):
        return tile_stats(block_terms(operands))

    partial_stats = lax.map(stats_block, blocked)
    local_stats = tuple((item.reshape(slab_rows) for item in partial_stats))
    slab_stats = jax.tree.map(lambda part: of_everyone(part, DEV), local_stats)
    own_stats = tuple(
        (lax.dynamic_slice_in_dim(item, member_index * row_count, row_count) for item in slab_stats)
    )
    contrast, relation = row_losses(own_stats)
    loss_totals = (
        one_axis_at_a_time(jnp.sum(contrast), GRP_DEV),
        one_axis_at_a_time(jnp.sum(relation), GRP_DEV),
    )
    supcon_loss = loss_totals[0] / view_count
    relation_loss = loss_totals[1] / view_count
    blocked_stats = tuple(
        (item.reshape(block_total, block_rows) for item in coef_inputs(slab_stats))
    )
    gathered_stats = jax.tree.map(lambda part: gathered_copies(part, GRP, 0), own_stats)
    key_stats = coef_inputs(gathered_stats)

    def pair_block(operands):
        terms = block_terms(operands)
        row_part = coefficient(
            terms,
            operands[4][:, None],
            operands[5][:, None],
            operands[6][:, None],
            operands[7][:, None],
        ).astype(jnp.bfloat16)
        column_part = coefficient(
            terms,
            key_stats[0][None, :],
            key_stats[1][None, :],
            key_stats[2][None, :],
            key_stats[3][None, :],
        ).astype(jnp.bfloat16)
        return (row_part, column_part)

    row_coef, column_coef = lax.map(pair_block, blocked + blocked_stats)
    row_coef = row_coef.reshape(slab_rows, key_count)
    column_coef = column_coef.reshape(slab_rows, key_count)
    first = lax.dot_general(
        row_coef, anchor_unit, (((0,), (0,)), ((), ())), preferred_element_type=jnp.float32
    )
    second = lax.dot_general(
        column_coef, anchor_unit, (((0,), (0,)), ((), ())), preferred_element_type=jnp.float32
    )
    grad = summed_on_arrival(first + second, GRP, 0)
    along = jnp.sum(unit_student * grad, axis=1, keepdims=True)
    feature_grad = scaling * (grad - unit_student * along)
    return (supcon_loss, relation_loss, feature_grad)


def solution(mesh):
    torus = Mesh(mesh.devices.reshape(2, 2, 4, 2, 4), ("grp_0", "grp_1", "dev_0", "dev_1", "dev_2"))
    return jax.shard_map(
        body,
        mesh=torus,
        in_specs=(P(GRP_DEV, None), P(GRP_DEV, None), P(GRP_DEV)),
        out_specs=(P(), P(), P(GRP_DEV, None)),
        check_vma=False,
    )
```

profile of v0, /device:TPU:1, one launch (start us, length us, event | category | flops | bytes accessed | tf_op | source)
XLA Modules:
  0.0 532.0 jit_solution(1962415202203950925)
XLA Ops:
  12.3 83.7 %all-gather = s32[32,1,128]{2,1,0:T(1,128)S(1)} all-gather(s32[1,1,128]{2,1,0:T(1,128)} %bitcast.156), channel_id=1, replica_groups=mesh['grp_0'=2,'grp_1'=2,'dev_0'=4,'dev_1'=2,'dev_2'=4] {'dev_0','dev_1'..., dimensions={0}, use_global_device_ids=true | all-gather | bytes 16896 | tf_op jit(solution)/shard_map/all_gather | solution.py:139
  97.2 19.8 %all-gather.1 = s32[4,1,128]{2,1,0:T(1,128)S(1)} all-gather(s32[1,1,128]{2,1,0:T(1,128)} %bitcast.157), channel_id=1, replica_groups=mesh['grp_0'=2,'grp_1'=2,'dev_0'=4,'dev_1'=2,'dev_2'=4] {'grp_0','grp_1'}, dimensions={0}, use_global_device_ids=true | all-gather | bytes 2560 | tf_op jit(solution)/shard_map/all_gather | solution.py:143
  118.8 85.0 %all-gather.5.cloned.1.call-done = bf16[4096,2048]{1,0:T(8,128)(2,1)} async-done(((bf16[128,2048]{1,0:T(8,128)(2,1)}), bf16[4096,2048]{1,0:T(8,128)(2,1)}) %all-gather.5.cloned.1.call-update) | async-done | bytes 16777232 | tf_op jit(solution)/shard_map/all_gather | solution.py:24
  203.8 11.6 %fusion.43 = (bf16[4096,1024]{1,0:T(8,128)(2,1)}, bf16[4096,1024]{1,0:T(8,128)(2,1)}) fusion(bf16[4096,2048]{1,0:T(8,128)(2,1)} %all-gather.5.cloned.1.call-done), kind=kLoop, calls=%fused_computation.85 | loop fusion | bytes 33554432 | tf_op jit(solution)/shard_map/split | solution.py:25
  215.4 41.0 %while.40 = (s32[]{:T(128)}, f32[8,512]{1,0:T(8,128)S(1)}, f32[8,512]{1,0:T(8,128)S(1)}, f32[8,512]{1,0:T(8,128)S(1)}, f32[8,512]{1,0:T(8,128)S(1)}, /*index=5*/...) while((s32[]{:T(128)}, f32[8,512]{1,0:T(8,128)S(1)}, ...), condition=%wide.region_9.10_spmd.clone, body=%wide.region_2.9_spmd.clone.sunk | while | flops 1079244288 | bytes 6352073 | solution.py:179
  217.6 2.6 select_reduce_fusion.2
  222.7 2.6 select_reduce_fusion.2
  227.8 2.6 select_reduce_fusion.2
  233.0 2.6 select_reduce_fusion.2
  238.1 2.6 select_reduce_fusion.2
  243.2 2.6 select_reduce_fusion.2
  248.4 2.6 select_reduce_fusion.2
  253.5 2.6 select_reduce_fusion.2
  258.0 5.4 %all-to-all-start.4 = ((f32[32,1,4096]{2,1,0:T(1,128)}), f32[32,1,4096]{2,1,0:T(1,128)S(1)}, u32[]{:S(2)}, u32[]{:S(2)}) async-start(f32[32,1,4096]{2,1,0:T(1,128)} %broadcast_in_dim.125), calls=%async_computation.4 | async-start | bytes 1048576 | tf_op jit(solution)/shard_map/all_to_all | solution.py:30
  263.4 10.6 %all-to-all-done.4 = f32[32,1,4096]{2,1,0:T(1,128)S(1)} async-done(((f32[32,1,4096]{2,1,0:T(1,128)}), f32[32,1,4096]{2,1,0:T(1,128)S(1)}, u32[]{:S(2)}, u32[]{:S(2)}) %all-to-all-start.4) | async-done | bytes 524320 | tf_op jit(solution)/shard_map/all_to_all | solution.py:30
  275.4 5.9 %all-to-all-start.5 = ((f32[32,1,4096]{2,1,0:T(1,128)}), f32[32,1,4096]{2,1,0:T(1,128)S(1)}, u32[]{:S(2)}, u32[]{:S(2)}) async-start(f32[32,1,4096]{2,1,0:T(1,128)} %broadcast_in_dim.127), calls=%async_computation.5 | async-start | bytes 1048576 | tf_op jit(solution)/shard_map/all_to_all | solution.py:30
  281.3 10.7 %all-to-all-done.5 = f32[32,1,4096]{2,1,0:T(1,128)S(1)} async-done(((f32[32,1,4096]{2,1,0:T(1,128)}), f32[32,1,4096]{2,1,0:T(1,128)S(1)}, u32[]{:S(2)}, u32[]{:S(2)}) %all-to-all-start.5) | async-done | bytes 524320 | tf_op jit(solution)/shard_map/all_to_all | solution.py:30
  293.3 6.0 %all-to-all-start.3 = ((f32[32,1,4096]{2,1,0:T(1,128)}), f32[32,1,4096]{2,1,0:T(1,128)S(1)}, u32[]{:S(2)}, u32[]{:S(2)}) async-start(f32[32,1,4096]{2,1,0:T(1,128)} %broadcast_in_dim.123), calls=%async_computation.3 | async-start | bytes 1048576 | tf_op jit(solution)/shard_map/all_to_all | solution.py:30
  299.2 10.7 %all-to-all-done.3 = f32[32,1,4096]{2,1,0:T(1,128)S(1)} async-done(((f32[32,1,4096]{2,1,0:T(1,128)}), f32[32,1,4096]{2,1,0:T(1,128)S(1)}, u32[]{:S(2)}, u32[]{:S(2)}) %all-to-all-start.3) | async-done | bytes 524320 | tf_op jit(solution)/shard_map/all_to_all | solution.py:30
  311.1 6.0 %all-to-all-start.1 = ((f32[32,1,4096]{2,1,0:T(1,128)}), f32[32,1,4096]{2,1,0:T(1,128)S(1)}, u32[]{:S(2)}, u32[]{:S(2)}) async-start(f32[32,1,4096]{2,1,0:T(1,128)} %broadcast_in_dim.119), calls=%async_computation.1 | async-start | bytes 1048576 | tf_op jit(solution)/shard_map/all_to_all | solution.py:30
  317.1 10.7 %all-to-all-done.1 = f32[32,1,4096]{2,1,0:T(1,128)S(1)} async-done(((f32[32,1,4096]{2,1,0:T(1,128)}), f32[32,1,4096]{2,1,0:T(1,128)S(1)}, u32[]{:S(2)}, u32[]{:S(2)}) %all-to-all-start.1) | async-done | bytes 524320 | tf_op jit(solution)/shard_map/all_to_all | solution.py:30
  329.0 6.0 %all-to-all-start.2 = ((f32[32,1,4096]{2,1,0:T(1,128)}), f32[32,1,4096]{2,1,0:T(1,128)S(1)}, u32[]{:S(2)}, u32[]{:S(2)}) async-start(f32[32,1,4096]{2,1,0:T(1,128)} %broadcast_in_dim.121), calls=%async_computation.2 | async-start | bytes 1048576 | tf_op jit(solution)/shard_map/all_to_all | solution.py:30
  335.0 10.7 %all-to-all-done.2 = f32[32,1,4096]{2,1,0:T(1,128)S(1)} async-done(((f32[32,1,4096]{2,1,0:T(1,128)}), f32[32,1,4096]{2,1,0:T(1,128)S(1)}, u32[]{:S(2)}, u32[]{:S(2)}) %all-to-all-start.2) | async-done | bytes 524320 | tf_op jit(solution)/shard_map/all_to_all | solution.py:30
  346.9 6.0 %all-to-all-start = ((f32[32,1,4096]{2,1,0:T(1,128)}), f32[32,1,4096]{2,1,0:T(1,128)S(1)}, u32[]{:S(2)}, u32[]{:S(2)}) async-start(f32[32,1,4096]{2,1,0:T(1,128)} %broadcast_in_dim.117), calls=%async_computation | async-start | bytes 1048576 | tf_op jit(solution)/shard_map/all_to_all | solution.py:30
  354.7 8.8 %all-to-all-done = f32[32,1,4096]{2,1,0:T(1,128)S(1)} async-done(((f32[32,1,4096]{2,1,0:T(1,128)}), f32[32,1,4096]{2,1,0:T(1,128)S(1)}, u32[]{:S(2)}, u32[]{:S(2)}) %all-to-all-start) | async-done | bytes 524320 | tf_op jit(solution)/shard_map/all_to_all | solution.py:30
  364.1 6.4 %all-to-all-start.8 = ((f32[4,1,128]{2,1,0:T(1,128)}), f32[4,1,128]{2,1,0:T(1,128)S(1)}, u32[]{:S(2)}, u32[]{:S(2)}) async-start(f32[4,1,128]{2,1,0:T(1,128)} %broadcast_in_dim.130), calls=%async_computation.8 | async-start | bytes 4096 | tf_op jit(solution)/shard_map/all_to_all | solution.py:30
  374.1 3.9 all-to-all-start.9
  381.6 3.9 all-to-all-start.7
  385.5 3.0 all-to-all-done.7
  389.1 3.9 all-to-all-start.6
  393.0 3.0 all-to-all-done.6
  396.0 52.6 %while.41 = (s32[]{:T(128)}, bf16[8,512,512]{2,1,0:T(8,128)(2,1)}, bf16[8,512,512]{2,1,0:T(8,128)(2,1)}, s32[8,512]{1,0:T(8,128)S(1)}, bf16[8,512,1024]{2,1,0:T(...) while((s32[]{:T(128)}, bf16[8,512,512]{2,1,0:T(8,128)(2,1)}, ...), condition=%wide.region_29.30_spmd.clone, body=%wide.region_28.29_spmd.clone.sunk | while | flops 1082130944 | bytes 7392977 | solution.py:216
  398.4 4.2 bitcast_dynamic-update-slice_fusion.3
  405.0 4.2 bitcast_dynamic-update-slice_fusion.3
  411.6 4.2 bitcast_dynamic-update-slice_fusion.3
  418.1 4.2 bitcast_dynamic-update-slice_fusion.3
  424.7 4.2 bitcast_dynamic-update-slice_fusion.3
  431.3 4.2 bitcast_dynamic-update-slice_fusion.3
  437.9 4.1 bitcast_dynamic-update-slice_fusion.3
  444.4 4.2 bitcast_dynamic-update-slice_fusion.3
  448.6 8.4 %fusion.41 = f32[512,1024]{1,0:T(8,128)S(1)} fusion(bf16[4096,512]{1,0:T(8,128)(2,1)} %bitcast.166, bf16[4096,2048]{1,0:T(8,128)(2,1)} %all-gather.5.cloned.1.call-done), kind=kOutput, calls=%fused_computation.83 | convolution fusion | flops 4294967296 | bytes 14680064 | tf_op jit(solution)/shard_map/dot_general | solution.py:219
  457.0 8.9 %convolution_add_fusion.3 = f32[512,1024]{1,0:T(8,128)} fusion(f32[512,1024]{1,0:T(8,128)S(1)} %fusion.41, bf16[4096,512]{1,0:T(8,128)(2,1)S(1)} %bitcast.167, bf16[4096,2048]{1,0:T(8,128)(2,1)} %all-gather.5.cloned.1.call-done), kind=kOutput, calls=%fused_computation.57 | convolution fusion | flops 4295491584 | bytes 16777216 | tf_op jit(solution)/shard_map/dot_general | solution.py:222
  465.9 4.4 all-to-all-start.10
  470.3 25.3 %all-reduce.4 = (f32[]{:T(128)}, f32[]{:T(128)}) all-reduce(f32[]{:T(128)} %get-tuple-element.676, f32[]{:T(128)} %get-tuple-element.673), channel_id=1, replica_groups=mesh['grp_0'=2,'grp_1'=2,'dev_0'=4,'dev_1'=2,'dev_2'=4] {'grp_0'}, use_global_device_ids=true, to_apply=%region_14.15 | all-reduce | flops 2 | bytes 16 | tf_op jit(solution)/shard_map/psum | solution.py:38
  495.6 3.7 all-reduce.3
  499.3 7.5 %all-reduce.1 = (f32[]{:T(128)}, f32[]{:T(128)}) all-reduce(f32[]{:T(128)} %get-tuple-element.669, f32[]{:T(128)} %get-tuple-element.670), channel_id=1, replica_groups=mesh['grp_0'=2,'grp_1'=2,'dev_0'=4,'dev_1'=2,'dev_2'=4] {'dev_0'}, use_global_device_ids=true, to_apply=%region_16.17 | all-reduce | flops 2 | bytes 16 | tf_op jit(solution)/shard_map/psum | solution.py:38
  506.7 5.9 %all-reduce.2 = (f32[]{:T(128)}, f32[]{:T(128)}) all-reduce(f32[]{:T(128)} %get-tuple-element.665, f32[]{:T(128)} %get-tuple-element.666), channel_id=1, replica_groups=mesh['grp_0'=2,'grp_1'=2,'dev_0'=4,'dev_1'=2,'dev_2'=4] {'dev_1'}, use_global_device_ids=true, to_apply=%region_17.18 | all-reduce | flops 2 | bytes 16 | tf_op jit(solution)/shard_map/psum | solution.py:38
  512.6 7.5 %all-reduce = (f32[]{:T(128)}, f32[]{:T(128)}) all-reduce(f32[]{:T(128)} %get-tuple-element.667, f32[]{:T(128)} %get-tuple-element.668), channel_id=1, replica_groups=mesh['grp_0'=2,'grp_1'=2,'dev_0'=4,'dev_1'=2,'dev_2'=4] {'dev_2'}, use_global_device_ids=true, to_apply=%region_18.19 | all-reduce | flops 2 | bytes 16 | tf_op jit(solution)/shard_map/psum | solution.py:38
  (181 shorter events, 66.3 us)
Async XLA Ops:
  7.2 109.9 %all-gather.7.cloned.1.call-start = ((), (), s32[]{:S(2)}) async-start(), calls=%async_computation.12 | async-start | bytes 2621440 | tf_op jit(solution)/shard_map/all_gather | solution.py:24
  11.4 192.4 %all-gather.5.cloned.1.call-start = ((), (), s32[]{:S(2)}) async-start(), calls=%async_computation.11 | async-start | bytes 17301504 | tf_op jit(solution)/shard_map/all_gather | solution.py:24
  256.5 1.5 copy-start.1
  256.5 36.8 %copy-start.2 = (bf16[512,1024]{1,0:T(8,128)(2,1)}, bf16[512,1024]{1,0:T(8,128)(2,1)S(1)}, u32[]{:S(2)}) copy-start(bf16[512,1024]{1,0:T(8,128)(2,1)S(1)} %get-tuple-element.1066) | copy-start | bytes 3145732
  258.0 16.1 %all-to-all-start.4 = ((f32[32,1,4096]{2,1,0:T(1,128)}), f32[32,1,4096]{2,1,0:T(1,128)S(1)}, u32[]{:S(2)}, u32[]{:S(2)}) async-start(f32[32,1,4096]{2,1,0:T(1,128)} %broadcast_in_dim.125), calls=%async_computation.4 | async-start | bytes 1048576 | tf_op jit(solution)/shard_map/all_to_all | solution.py:30
  275.4 16.6 %all-to-all-start.5 = ((f32[32,1,4096]{2,1,0:T(1,128)}), f32[32,1,4096]{2,1,0:T(1,128)S(1)}, u32[]{:S(2)}, u32[]{:S(2)}) async-start(f32[32,1,4096]{2,1,0:T(1,128)} %broadcast_in_dim.127), calls=%async_computation.5 | async-start | bytes 1048576 | tf_op jit(solution)/shard_map/all_to_all | solution.py:30
  293.3 16.6 %all-to-all-start.3 = ((f32[32,1,4096]{2,1,0:T(1,128)}), f32[32,1,4096]{2,1,0:T(1,128)S(1)}, u32[]{:S(2)}, u32[]{:S(2)}) async-start(f32[32,1,4096]{2,1,0:T(1,128)} %broadcast_in_dim.123), calls=%async_computation.3 | async-start | bytes 1048576 | tf_op jit(solution)/shard_map/all_to_all | solution.py:30
  311.1 16.6 %all-to-all-start.1 = ((f32[32,1,4096]{2,1,0:T(1,128)}), f32[32,1,4096]{2,1,0:T(1,128)S(1)}, u32[]{:S(2)}, u32[]{:S(2)}) async-start(f32[32,1,4096]{2,1,0:T(1,128)} %broadcast_in_dim.119), calls=%async_computation.1 | async-start | bytes 1048576 | tf_op jit(solution)/shard_map/all_to_all | solution.py:30
  329.0 16.6 %all-to-all-start.2 = ((f32[32,1,4096]{2,1,0:T(1,128)}), f32[32,1,4096]{2,1,0:T(1,128)S(1)}, u32[]{:S(2)}, u32[]{:S(2)}) async-start(f32[32,1,4096]{2,1,0:T(1,128)} %broadcast_in_dim.121), calls=%async_computation.2 | async-start | bytes 1048576 | tf_op jit(solution)/shard_map/all_to_all | solution.py:30
  346.9 16.6 %all-to-all-start = ((f32[32,1,4096]{2,1,0:T(1,128)}), f32[32,1,4096]{2,1,0:T(1,128)S(1)}, u32[]{:S(2)}, u32[]{:S(2)}) async-start(f32[32,1,4096]{2,1,0:T(1,128)} %broadcast_in_dim.117), calls=%async_computation | async-start | bytes 1048576 | tf_op jit(solution)/shard_map/all_to_all | solution.py:30
  364.1 9.4 %all-to-all-start.8 = ((f32[4,1,128]{2,1,0:T(1,128)}), f32[4,1,128]{2,1,0:T(1,128)S(1)}, u32[]{:S(2)}, u32[]{:S(2)}) async-start(f32[4,1,128]{2,1,0:T(1,128)} %broadcast_in_dim.130), calls=%async_computation.8 | async-start | bytes 4096 | tf_op jit(solution)/shard_map/all_to_all | solution.py:30
  374.1 6.9 %all-to-all-start.9 = ((f32[4,1,128]{2,1,0:T(1,128)}), f32[4,1,128]{2,1,0:T(1,128)S(1)}, u32[]{:S(2)}, u32[]{:S(2)}) async-start(f32[4,1,128]{2,1,0:T(1,128)} %broadcast_in_dim.131), calls=%async_computation.9 | async-start | bytes 4096 | tf_op jit(solution)/shard_map/all_to_all | solution.py:30
  381.6 6.9 %all-to-all-start.7 = ((f32[4,1,128]{2,1,0:T(1,128)}), f32[4,1,128]{2,1,0:T(1,128)S(1)}, u32[]{:S(2)}, u32[]{:S(2)}) async-start(f32[4,1,128]{2,1,0:T(1,128)} %broadcast_in_dim.129), calls=%async_computation.7 | async-start | bytes 4096 | tf_op jit(solution)/shard_map/all_to_all | solution.py:30
  389.1 6.9 %all-to-all-start.6 = ((f32[4,1,128]{2,1,0:T(1,128)}), f32[4,1,128]{2,1,0:T(1,128)S(1)}, u32[]{:S(2)}, u32[]{:S(2)}) async-start(f32[4,1,128]{2,1,0:T(1,128)} %broadcast_in_dim.128), calls=%async_computation.6 | async-start | bytes 4096 | tf_op jit(solution)/shard_map/all_to_all | solution.py:30
  448.6 8.4 %copy-start.3 = (bf16[8,512,512]{2,1,0:T(8,128)(2,1)S(1)}, bf16[8,512,512]{2,1,0:T(8,128)(2,1)}, u32[]{:S(2)}) copy-start(bf16[8,512,512]{2,1,0:T(8,128)(2,1)} %get-tuple-element.514) | copy-start | bytes 12582916
  465.9 55.8 %copy-start = (bf16[128,1024]{1,0:T(8,128)(2,1)S(1)}, bf16[128,1024]{1,0:T(8,128)(2,1)}, u32[]{:S(2)}) copy-start(bf16[128,1024]{1,0:T(8,128)(2,1)} %param.7) | copy-start | bytes 786436
  465.9 55.6 %all-to-all-start.10 = ((f32[4,128,1024]{2,1,0:T(8,128)}), f32[4,128,1024]{2,1,0:T(8,128)S(1)}, u32[]{:S(2)}, u32[]{:S(2)}) async-start(f32[4,128,1024]{2,1,0:T(8,128)} %bitcast.128), calls=%async_computation.10 | async-start | bytes 4194304 | tf_op jit(solution)/shard_map/all_to_all | solution.py:59
Sparse Core Ops, SparseCore 0:
  11.6 32.8 all-gather.6
  48.2 155.6 all-gather.4
where the time goes:
time: 538 us; the launch traced here: 532 us
  waiting for transfers between devices  158 us (29%)
  blocking collectives  153 us (28%)
  matrix products  106 us (20%)
  starting transfers between devices  57.7 us (11%)
  local copies, waits for them, and re-layouts  27.3 us (5%)
  between operations  18 us (3%)
  other arithmetic  11 us (2%)
    dot_general x32, matrix products, inner_rows(): lax.dot_general(left, right, (((1,), (1,)), ((), ())), preferred_element_...  88.4 us
    all_gather x2, waiting for transfers between devices, side_by_side(): out = lax.all_gather(both, axis, axis=dim, tiled=True)  85.1 us
    all_gather x1, blocking collectives, body(): lax.all_gather(labels, DEV, axis=0, tiled=True)  83.7 us
    all_to_all x10, waiting for transfers between devices, sent_to_all(): return lax.all_to_all(copies, axis, split_axis=0, concat_axis=0, tiled=True)  72.3 us
    all_to_all x10, starting transfers between devices, sent_to_all(): return lax.all_to_all(copies, axis, split_axis=0, concat_axis=0, tiled=True)  53.3 us
    psum x5, blocking collectives, one_axis_at_a_time(): return functools.reduce(lax.psum, axes, value)  49.9 us
    all_gather x1, blocking collectives, body(): lax.all_gather(labels, GRP, axis=0, tiled=True)  19.8 us
    split x2, local copies, waits for them, and re-layouts, side_by_side(): jnp.split(out, [sum(widths[:k]) for k in range(1, len(widths))], axis=along)  13.3 us
  transfers between devices with their start and end apart: 13, of which 11 were waited for; matrix products, arithmetic and copies ran while one was open for 1% of the time, Pallas kernels for 0%

commit v1 on v0

v1 whole, which is shorter than its diff:
```python
import math

import jax
import jax.numpy as jnp
from jax import lax
from jax.experimental import pallas as pl
from jax.experimental.pallas import tpu as pltpu
from jax.sharding import Mesh
from jax.sharding import PartitionSpec as P

AXES = ("x_lo", "core", "z", "x_hi", "y")
MESH = pl.DeviceIdType.MESH
F32, BF16 = jnp.float32, jnp.bfloat16

temp_sup = 0.1
temp_student = 0.2
temp_teacher = 0.05
epsilon = 1e-06
LOG2E = math.log2(math.e)

KEY_POS = {2: 0, 1: 1, 3: 2, 0: 3}
RING = (1, 2, 3)


def plane_messages():
    out = {}
    out["u", (1, 0)] = ((0, 0), "y", -1)
    out["u", (3, 0)] = ((0, 0), "y", 1)
    out["v", (0, 1)] = ((0, 0), "z", -1)
    out["v", (0, 3)] = ((0, 0), "z", 1)
    out["u", (2, 0)] = ((1, 0), "y", -1)
    out["v", (0, 2)] = ((0, 3), "z", 1)
    for d in range(4):
        out["u", (d, 1)] = ((d, 0), "z", -1)
        out["u", (d, 3)] = ((d, 0), "z", 1)
        out["u", (d, 2)] = ((d, 1), "z", -1) if d in (0, 3) else ((d, 3), "z", 1)
        out["v", (1, d)] = ((0, d), "y", -1)
        out["v", (3, d)] = ((0, d), "y", 1)
        out["v", (2, d)] = ((1, d), "y", -1) if d in (3,) else ((3, d), "y", 1)
    return out


def line_messages():
    return {
        ("ku", 1): (0, "x", -1),
        ("ku", 3): (0, "x", 1),
        ("kv", 1): (0, "x", -1),
        ("kv", 3): (0, "x", 1),
        ("ku", 2): (1, "x", -1),
        ("kv", 2): (3, "x", 1),
    }


def make_schedule():
    wire, hop, tile, local = 5.6, 2.2, 1.3, 1.4
    messages = {**plane_messages(), **line_messages()}
    free = {}
    arrive = {}

    def launch(name, when):
        _, axis, step = messages[name]
        begin = max(free.get((axis, step), 0.0), when)
        free[axis, step] = begin + wire
        arrive[name] = begin + wire + hop

    def after(kind, slot):
        return [n for n, m in messages.items() if n[0] == kind and m[0] == slot]

    first = []
    for kind, own in (("u", (0, 0)), ("v", (0, 0)), ("ku", 0), ("kv", 0)):
        first += after(kind, own)
    order = {n: i for i, n in enumerate(messages)}
    first.sort(key=lambda n: order[n])
    for name in first:
        launch(name, 0.0)
    now, waited, done_tiles = 0.0, {}, []
    sequence = [("launch", tuple(first))]
    pending_actions = []
    steps = []
    slots = [(dy, dz) for dz in range(4) for dy in range(4)]
    have = {("u", (0, 0)): 0.0, ("v", (0, 0)): 0.0}
    while len(done_tiles) < 16:
        coming = sorted((t, order[n], n) for n, t in arrive.items() if n not in waited)
        keys_in = all(n in waited for n in line_messages())
        ready = []
        if keys_in:
            ready = [
                s
                for s in slots
                if s not in done_tiles
                and all((k, s) in have and have[k, s] + local <= now for k in ("u", "v"))
            ]
        if coming and coming[0][0] <= now or (coming and not ready):
            t, _, name = coming[0]
            now = max(now, t) + 0.05
            waited[name] = now
            follow = after(name[0], name[1])
            for f in follow:
                launch(f, now)
            if name[0] in ("u", "v"):
                have[name] = now
            pending_actions.append((name, tuple(follow)))
        elif ready:
            ready.sort(key=lambda s: (max(have["u", s], have["v", s]), slots.index(s)))
            done_tiles.append(ready[0])
            steps.append(tuple(pending_actions))
            pending_actions = []
            now += tile
        else:
            now = min(
                max(have["u", s], have["v", s]) + local + 1e-6
                for s in slots
                if s not in done_tiles and ("u", s) in have and ("v", s) in have
            )
    return tuple(first), tuple(steps), tuple(done_tiles), now


FIRST, STEPS, TILES, _ = make_schedule()
SLOT = {s: k for k, s in enumerate(TILES)}
MESSAGES = {**plane_messages(), **line_messages()}
NAMES = (
    list(MESSAGES)
    + [("pu", s) for s in TILES]
    + [("pv", s) for s in TILES]
    + [(kind, d) for kind in ("lx", "ly", "lz", "sx", "sy", "sz", "ox") for d in RING]
    + [("lp", 0), ("sp", 0)]
    + [("r", i) for i in range(6)]
)
IDS = {n: i for i, n in enumerate(NAMES)}


def kernel(
    student_ref,
    teacher_ref,
    label_ref,
    grad_ref,
    loss_ref,
    ua,
    va,
    uk,
    vk,
    raw_s,
    raw_t,
    signed_b,
    w_all,
    acc,
    key_label,
    anchor_label,
    label_plane,
    label_line,
    part,
    part_in,
    coef_plane,
    key_coef,
    anchor_coef,
    loss_line,
    gbuf,
    total,
    relay,
    arrive,
    send_sem,
    recv_sem,
):
    rows, width = student_ref.shape
    x_lo, x_hi = lax.axis_index("x_lo"), lax.axis_index("x_hi")
    core = lax.axis_index("core")
    y, z = lax.axis_index("y"), lax.axis_index("z")
    x = x_hi * 2 + x_lo
    pair = 2 * rows

    def device(axis, step):
        if axis == "core":
            return {"core": 1 - core}
        if axis == "x":
            there = lax.rem(x + step + 4, 4)
            return {"x_hi": there // 2, "x_lo": lax.rem(there, 2)}
        place = y if axis == "y" else z
        return {axis: lax.rem(place + step + 4, 4)}

    def key_rows(d):
        return pl.ds(KEY_POS[d] * rows, rows)

    def own_rows(slot):
        return pl.ds(SLOT[slot] * pair, rows)

    half = rows // 2

    def refs_of(name):
        kind, slot = name
        if kind in ("u", "v"):
            source, axis, step = MESSAGES[name]
            buf = ua if kind == "u" else va
            return buf.at[own_rows(source)], buf.at[own_rows(slot)], axis, step
        if kind in ("ku", "kv"):
            source, axis, step = MESSAGES[name]
            buf = uk if kind == "ku" else vk
            return buf.at[key_rows(source)], buf.at[key_rows(slot)], axis, step
        if kind in ("pu", "pv"):
            buf = ua if kind == "pu" else va
            there = pl.ds(SLOT[slot] * pair + rows, rows)
            return buf.at[own_rows(slot)], buf.at[there], "core", 0
        if kind in ("lx", "ox"):
            buf = label_line if kind == "lx" else loss_line
            return buf.at[0], buf.at[slot], "x", -slot
        if kind == "sx":
            return part, part_in.at[slot - 1], "x", -slot
        plane = label_plane if kind[0] == "l" else coef_plane
        if kind in ("ly", "sy"):
            return plane.at[0, 0, 0], plane.at[0, 0, slot], "y", -slot
        if kind in ("lz", "sz"):
            return plane.at[0, 0], plane.at[0, slot], "z", -slot
        if kind in ("lp", "sp"):
            return plane.at[0], plane.at[1], "core", 0
        two, nxt, prv = KEY_POS[2] * rows, KEY_POS[1] * rows, KEY_POS[3] * rows
        return (
            (total.at[pl.ds(two, half)], relay.at[0], "x", 1),
            (total.at[pl.ds(two + half, half)], relay.at[1], "x", -1),
            (total.at[pl.ds(nxt + half, half)], arrive.at[0, pl.ds(half, half)], "x", 1),
            (total.at[pl.ds(prv, half)], arrive.at[1, pl.ds(0, half)], "x", -1),
            (total.at[pl.ds(nxt, half)], arrive.at[0, pl.ds(0, half)], "x", 1),
            (total.at[pl.ds(prv + half, half)], arrive.at[1, pl.ds(half, half)], "x", -1),
        )[slot]

    def message(name):
        source, target, axis, step = refs_of(name)
        return pltpu.make_async_remote_copy(
            src_ref=source,
            dst_ref=target,
            send_sem=send_sem.at[IDS[name]],
            recv_sem=recv_sem.at[IDS[name]],
            device_id=device(axis, step),
            device_id_type=MESH,
        )

    def start(*names):
        for name in names:
            message(name).start()

    def arrived(*names):
        for name in names:
            message(name).wait_recv()

    barrier = pltpu.get_barrier_semaphore()
    for axis in ("x", "y", "z"):
        for d in RING:
            pl.semaphore_signal(barrier, inc=1, device_id=device(axis, d), device_id_type=MESH)
    pl.semaphore_signal(barrier, inc=1, device_id=device("core", 0), device_id_type=MESH)

    own_key = KEY_POS[0] * rows

    def normalise(i, carry):
        here = pl.ds(pl.multiple_of(i * 16, 16), 16)
        there = pl.ds(pl.multiple_of(own_key + i * 16, 16), 16)
        for raw, anchors, keys in ((student_ref, ua, uk), (teacher_ref, va, vk)):
            values = raw[here, :].astype(F32)
            scaling = lax.rsqrt(jnp.sum(values * values, axis=1, keepdims=True) + epsilon)
            unit = (values * scaling).astype(BF16)
            anchors[here, :] = unit
            keys[there, :] = unit
        return carry

    lax.fori_loop(0, rows // 16, normalise, 0)
    own_label = jnp.broadcast_to(label_ref[...].astype(F32), (8, rows))
    label_plane[0, 0, 0] = own_label
    label_line[0] = own_label
    acc[...] = jnp.zeros_like(acc)
    pl.semaphore_wait(barrier, 10)

    start(*[("ly", d) for d in RING], *[("lx", d) for d in RING])
    start(*FIRST)
    start(("pu", (0, 0)), ("pv", (0, 0)))
    arrived(*[("ly", d) for d in RING])
    start(*[("lz", d) for d in RING])
    arrived(*[("lx", d) for d in RING])
    for d in range(4):
        line = label_line[d][0:1]
        key_label[key_rows(d), :] = jnp.broadcast_to(line, (rows, rows)).T
    arrived(*[("lz", d) for d in RING])
    start(("lp", 0))
    arrived(("lp", 0))
    for (dy, dz), k in SLOT.items():
        for c in range(2):
            anchor_label[:, pl.ds(k * pair + c * rows, rows)] = label_plane[c, dz, dy]

    chunk = 32
    k_rel = LOG2E / temp_student
    k_tea = LOG2E / temp_teacher

    def elementwise(k, count, base, diagonal):
        def one(i, carry):
            r = pl.ds(pl.multiple_of(base + i * chunk, chunk), chunk)
            label = key_label[r, :]
            sums = [None] * 6
            for c in range(2):
                lanes = pl.ds(c * rows, rows)
                columns = pl.ds(pl.multiple_of(k * pair + c * rows, rows), rows)
                s = raw_s[r, lanes]
                t = raw_t[r, lanes]
                b = jnp.exp2(s * k_rel - k_rel)
                w = jnp.exp2(t * k_tea - k_tea)
                same = label == jnp.broadcast_to(anchor_label[0:1, columns], label.shape)
                if diagonal and c == 0:
                    row = lax.broadcasted_iota(jnp.int32, label.shape, 0) + i * chunk
                    lane = lax.broadcasted_iota(jnp.int32, label.shape, 1)
                    other = row != lane
                    same = jnp.logical_and(same, other)
                    b = jnp.where(other, b, 0.0)
                    w = jnp.where(other, w, 0.0)
                signed_b[r, columns] = jnp.where(same, -b, b)
                w_all[r, columns] = w
                values = (b * b, b, w, w * s, jnp.where(same, s, 0.0), jnp.where(same, 1.0, 0.0))
                sums = [v if p is None else p + v for p, v in zip(sums, values)]
            for n in range(6):
                acc[n, r, :] += sums[n]
            return carry

        lax.fori_loop(0, count // chunk, one, 0)

    key_count = 4 * rows
    contract = (((1,), (1,)), ((), ()))

    def tile_step(k, carry):
        for n, actions in enumerate(STEPS):
            @pl.when(k == n)
            def _(n=n, actions=actions):
                for name, follow in actions:
                    arrived(name)
                    start(*follow)
                    if name[0] in ("u", "v"):
                        start(("p" + name[0], name[1]))
                arrived(("pu", TILES[n]), ("pv", TILES[n]))

        here = pl.ds(pl.multiple_of(k * pair, pair), pair)
        raw_s[...] = lax.dot_general(uk[...], ua[here, :], contract, preferred_element_type=F32)
        raw_t[...] = lax.dot_general(vk[...], va[here, :], contract, preferred_element_type=F32)
        elementwise(k, key_count - rows, 0, False)

        @pl.when(k == 0)
        def _():
            elementwise(k, rows, own_key, True)

        @pl.when(k > 0)
        def _():
            elementwise(k, rows, own_key, False)

        return carry

    lax.fori_loop(0, 16, tile_step, 0)

    lane = lax.broadcasted_iota(jnp.int32, (rows, rows), 1)
    for d in range(4):
        packed = jnp.zeros((rows, rows), F32)
        for n in range(6):
            packed = jnp.where(
                lane == n, jnp.sum(acc[n, key_rows(d), :], axis=1, keepdims=True), packed
            )
        part[d] = packed.T[0:8]
    start(*[("sx", d) for d in RING])
    arrived(*[("sx", d) for d in RING])
    line = lax.broadcasted_iota(jnp.int32, (8, rows), 0)
    for e in range(4):
        sums = part[e]
        for d in RING:
            sums = sums + part_in[d - 1, (e - d) % 4]
        sup, rel, tea = sums[0:1], sums[1:2], sums[2:3]
        positives = jnp.maximum(sums[5:6], 1.0)
        coefs = (
            (1.0 / temp_sup) / sup,
            (1.0 / temp_student) / rel,
            (1.0 / temp_student) / tea,
            (1.0 / temp_sup) / positives,
        )
        for n in range(4):
            key_coef[n, key_rows(e), :] = jnp.broadcast_to(coefs[n], (rows, rows)).T
        if e == 0:
            contrast = (1.0 - sums[4:5] / positives) / temp_sup + jnp.log(sup)
            relation = (1.0 - sums[3:4] / tea) / temp_student + jnp.log(rel)
            mine = jnp.zeros((8, rows), F32)
            for n, value in enumerate((*coefs, contrast, relation)):
                mine = jnp.where(line == n, jnp.broadcast_to(value, (8, rows)), mine)
            coef_plane[0, 0, 0] = mine
            start(*[("sy", d) for d in RING])

    depth = 4 * rows
    chunks = 32 * rows // depth

    def fill(c, first, count, side):
        def one(i, carry):
            r = pl.ds(pl.multiple_of(first + i * chunk, chunk), chunk)
            g = pl.ds(pl.multiple_of(i * chunk, chunk), chunk)
            for q in range(depth // rows):
                columns = pl.ds(pl.multiple_of(c * depth + q * rows, rows), rows)
                sb = signed_b[r, columns]
                w = w_all[r, columns]
                if side == "key":
                    ca, cb, cw, cp = [key_coef[n, r, :] for n in range(4)]
                else:
                    ca, cb, cw, cp = [
                        jnp.broadcast_to(anchor_coef[n : n + 1, columns], sb.shape)
                        for n in range(4)
                    ]
                value = (sb * sb * ca - jnp.where(sb < 0.0, cp, 0.0)) + (
                    jnp.abs(sb) * cb - w * cw
                )
                gbuf[g, pl.ds(q * rows, rows)] = value.astype(BF16)
            return carry

        lax.fori_loop(0, count // chunk, one, 0)

    def multiply(c, first, count, fresh):
        anchors = ua[pl.ds(pl.multiple_of(c * depth, depth), depth), :]
        product = jnp.dot(gbuf[pl.ds(0, count), :], anchors, preferred_element_type=F32)
        if fresh:
            total[pl.ds(first, count), :] = product
        else:
            total[pl.ds(first, count), :] += product

    def key_side(c, carry):
        @pl.when(c == 2)
        def _():
            arrived(*[("sy", d) for d in RING])
            start(*[("sz", d) for d in RING])

        @pl.when(c == 5)
        def _():
            arrived(*[("sz", d) for d in RING])
            start(("sp", 0))

        fill(c, 0, key_count, "key")
        multiply(c, 0, key_count, False)
        return carry

    total[...] = jnp.zeros_like(total)
    lax.fori_loop(0, chunks, key_side, 0)
    arrived(("sp", 0))
    for (dy, dz), k in SLOT.items():
        for c in range(2):
            anchor_coef[:, pl.ds(k * pair + c * rows, rows)] = coef_plane[c, dz, dy]
    losses = jnp.zeros((8, rows), F32)
    for cc in range(2):
        for zz in range(4):
            for yy in range(4):
                losses = losses + coef_plane[
                    lax.rem(cc + core, 2), lax.rem(zz + 4 - z, 4), lax.rem(yy + 4 - y, 4)
                ]
    loss_line[0] = losses
    start(*[("ox", d) for d in RING])

    def anchor_side(first, count):
        def one(c, carry):
            fill(c, first, count, "anchor")
            multiply(c, first, count, False)
            return carry

        lax.fori_loop(0, chunks, one, 0)

    anchor_side(0, rows)
    start(("r", 0), ("r", 1))
    anchor_side(rows, 2 * rows)
    start(("r", 2), ("r", 3))
    arrived(("r", 0))
    total[pl.ds(KEY_POS[1] * rows, half), :] += relay[0]
    start(("r", 4))
    arrived(("r", 1))
    total[pl.ds(KEY_POS[3] * rows + half, half), :] += relay[1]
    start(("r", 5))
    anchor_side(own_key, rows)

    arrived(*[("ox", d) for d in RING])
    sums = jnp.zeros((8, rows), F32)
    for xx in range(4):
        sums = sums + loss_line[lax.rem(xx + 4 - x, 4)]
    views = 128.0 * rows
    loss_ref[...] = jnp.broadcast_to(jnp.sum(sums, axis=1, keepdims=True), (8, rows)) / views

    arrived(("r", 2), ("r", 3), ("r", 4), ("r", 5))

    def finish(i, carry):
        here = pl.ds(pl.multiple_of(i * 16, 16), 16)
        there = pl.ds(pl.multiple_of(own_key + i * 16, 16), 16)
        values = student_ref[here, :].astype(F32)
        scaling = lax.rsqrt(jnp.sum(values * values, axis=1, keepdims=True) + epsilon)
        unit = values * scaling
        grad = total[there, :] + arrive[0, here, :] + arrive[1, here, :]
        along = jnp.sum(unit * grad, axis=1, keepdims=True)
        grad_ref[here, :] = scaling * (grad - unit * along)
        return carry

    lax.fori_loop(0, rows // 16, finish, 0)
    for name in NAMES:
        message(name).wait_send()


def body(student, teacher, labels):
    rows, width = student.shape
    keys, anchors = 4 * rows, 32 * rows
    vmem = pl.BlockSpec(memory_space=pltpu.VMEM)
    grad, losses = pl.pallas_call(
        kernel,
        out_shape=(
            jax.ShapeDtypeStruct((rows, width), F32),
            jax.ShapeDtypeStruct((8, rows), F32),
        ),
        in_specs=[vmem] * 3,
        out_specs=(vmem, vmem),
        scratch_shapes=[
            pltpu.VMEM((anchors, width), BF16),
            pltpu.VMEM((anchors, width), BF16),
            pltpu.VMEM((keys, width), BF16),
            pltpu.VMEM((keys, width), BF16),
            pltpu.VMEM((keys, 2 * rows), F32),
            pltpu.VMEM((keys, 2 * rows), F32),
            pltpu.VMEM((keys, anchors), F32),
            pltpu.VMEM((keys, anchors), F32),
            pltpu.VMEM((6, keys, rows), F32),
            pltpu.VMEM((keys, rows), F32),
            pltpu.VMEM((8, anchors), F32),
            pltpu.VMEM((2, 4, 4, 8, rows), F32),
            pltpu.VMEM((4, 8, rows), F32),
            pltpu.VMEM((4, 8, rows), F32),
            pltpu.VMEM((3, 4, 8, rows), F32),
            pltpu.VMEM((2, 4, 4, 8, rows), F32),
            pltpu.VMEM((4, keys, rows), F32),
            pltpu.VMEM((8, anchors), F32),
            pltpu.VMEM((4, 8, rows), F32),
            pltpu.VMEM((keys, 4 * rows), BF16),
            pltpu.VMEM((keys, width), F32),
            pltpu.VMEM((2, rows // 2, width), F32),
            pltpu.VMEM((2, rows, width), F32),
            pltpu.SemaphoreType.DMA((len(NAMES),)),
            pltpu.SemaphoreType.DMA((len(NAMES),)),
        ],
        compiler_params=pltpu.CompilerParams(
            collective_id=0, has_side_effects=True, vmem_limit_bytes=60 * 1024 * 1024
        ),
    )(student, teacher, labels.reshape(1, rows))
    return losses[4, 0], losses[5, 0], grad


def solution(mesh):
    torus = Mesh(mesh.devices.reshape(2, 2, 4, 2, 4), AXES)
    own = ("x_lo", "core", "z", "x_hi", "y")
    return jax.shard_map(
        body,
        mesh=torus,
        in_specs=(P(own, None), P(own, None), P(own)),
        out_specs=(P(), P(), P(own, None)),
        check_vma=False,
    )
```

time: 538 us -> 108 us (0.20); the launches traced: 532 us -> 108 us
  waiting for transfers between devices: 158 us -> 0 us
  blocking collectives: 153 us -> 0 us
  matrix products: 106 us -> 0 us
  Pallas kernels: 0 us -> 104 us
  starting transfers between devices: 57.7 us -> 0 us
  local copies, waits for them, and re-layouts: 27.3 us -> 3.16 us
  between operations: 18 us -> 0.64 us
  other arithmetic: 11 us -> 0 us
    dot_general x34 -> x0, matrix products: 106 us -> none  [the longest x32 88.4 us: inner_rows(): lax.dot_general(left, right, (((1,), (1,)), ((), ())), preferred_element_...]
    pallas_call x0 -> x1, Pallas kernels: none -> 104 us  [body(): pl.pallas_call(kernel, out_shape=(jax.ShapeDtypeStruct((rows, width), F32...]
    all_gather x2 -> x0, blocking collectives: 104 us -> none  [the longest x1 83.7 us: body(): lax.all_gather(labels, DEV, axis=0, tiled=True)]
    all_gather x2 -> x0, waiting for transfers between devices: 85.1 us -> none  [side_by_side(): out = lax.all_gather(both, axis, axis=dim, tiled=True)]
    all_to_all x11 -> x0, waiting for transfers between devices: 72.3 us -> none  [the longest x10 72.3 us: sent_to_all(): return lax.all_to_all(copies, axis, split_axis=0, concat_axis=0, tiled=True)]
    all_to_all x11 -> x0, starting transfers between devices: 57.7 us -> none  [the longest x10 53.3 us: sent_to_all(): return lax.all_to_all(copies, axis, split_axis=0, concat_axis=0, tiled=True)]
    psum x5 -> x0, blocking collectives: 49.9 us -> none  [one_axis_at_a_time(): return functools.reduce(lax.psum, axes, value)]
    split x2 -> x0, local copies, waits for them, and re-layouts: 13.3 us -> none  [side_by_side(): jnp.split(out, [sum(widths[:k]) for k in range(1, len(widths))], axis=along)]
  transfers between devices with their start and end apart: 13 -> 0, of which waited for: 11 -> 0; matrix products, arithmetic and copies ran while one was open for 1% -> 0% of each run, Pallas kernels for 0% -> 0%
where the time goes in v1:
time: 108 us
  Pallas kernels  104 us (96%)
  local copies, waits for them, and re-layouts  3.16 us (3%)
    pallas_call x1, Pallas kernels, body(): pl.pallas_call(kernel, out_shape=(jax.ShapeDtypeStruct((rows, width), F32...  104 us

profile of v1, /device:TPU:1, one launch (start us, length us, event | category | flops | bytes accessed | tf_op | source)
XLA Modules:
  0.0 107.7 jit_solution(5169443565494005372)
XLA Ops:
  0.6 103.9 %shard_map.58 = (f32[128,1024]{1,0:T(8,128)}, f32[8,128]{1,0:T(8,128)}) custom-call(bf16[128,1024]{1,0:T(8,128)(2,1)} %student_ref.1, bf16[128,1024]{1,0:T(8,128)(2,1)} %teacher_ref.1, s32[1,128]{1,0:T(1,128)} %bitcast.3), custom_call_target="tpu_custom_call" | custom-call | tf_op jit(solution)/shard_map/pallas_call | solution.py:498
  104.5 1.3 %fusion = (f32[1,1]{1,0:T(1,128)}, f32[1,1]{1,0:T(1,128)}) fusion(f32[8,128]{1,0:T(8,128)} %get-tuple-element.5), kind=kLoop, calls=%fused_computation | loop fusion | bytes 16 | tf_op jit(solution)/shard_map/slice | solution.py:537
  105.8 1.9 %copy.7 = f32[128,1024]{1,0:T(8,128)} copy(f32[128,1024]{1,0:T(8,128)} %get-tuple-element.14) | data formatting | bytes 1048576

commit v2 on v1

--- a/solution.py
+++ b/solution.py
@@ -20,109 +20,117 @@
 
 KEY_POS = {2: 0, 1: 1, 3: 2, 0: 3}
 RING = (1, 2, 3)
+OTHERS = [(dy, dz) for dz in range(4) for dy in range(4) if (dy, dz) != (0, 0)]
 
 
 def plane_messages():
     out = {}
-    out["u", (1, 0)] = ((0, 0), "y", -1)
-    out["u", (3, 0)] = ((0, 0), "y", 1)
-    out["v", (0, 1)] = ((0, 0), "z", -1)
-    out["v", (0, 3)] = ((0, 0), "z", 1)
-    out["u", (2, 0)] = ((1, 0), "y", -1)
-    out["v", (0, 2)] = ((0, 3), "z", 1)
-    for d in range(4):
-        out["u", (d, 1)] = ((d, 0), "z", -1)
-        out["u", (d, 3)] = ((d, 0), "z", 1)
-        out["u", (d, 2)] = ((d, 1), "z", -1) if d in (0, 3) else ((d, 3), "z", 1)
-        out["v", (1, d)] = ((0, d), "y", -1)
-        out["v", (3, d)] = ((0, d), "y", 1)
-        out["v", (2, d)] = ((1, d), "y", -1) if d in (3,) else ((3, d), "y", 1)
+    near = ((1, -1), (3, 1))
+
+    def along(kind, axis, others):
+        for d, step in near:
+            for o in others:
+                slot, source = ((d, o), (0, o)) if axis == "y" else ((o, d), (o, 0))
+                for h in range(2):
+                    out[kind, slot, h] = (source, axis, step)
+        for o in others:
+            for h, (d, step) in enumerate(near):
+                slot, source = ((2, o), (d, o)) if axis == "y" else ((o, 2), (o, d))
+                out[kind, slot, h] = (source, axis, step)
+
+    along("u", "y", (0,))
+    along("v", "z", (0,))
+    along("u", "z", range(4))
+    along("v", "y", range(4))
     return out
 
 
 def line_messages():
-    return {
-        ("ku", 1): (0, "x", -1),
-        ("ku", 3): (0, "x", 1),
-        ("kv", 1): (0, "x", -1),
-        ("kv", 3): (0, "x", 1),
-        ("ku", 2): (1, "x", -1),
-        ("kv", 2): (3, "x", 1),
-    }
+    out = {}
+    for kind in ("ku", "kv"):
+        for d, step in ((1, -1), (3, 1)):
+            for h in range(2):
+                out[kind, d, h] = (0, "x", step)
+        for h, (d, step) in enumerate(((1, -1), (3, 1))):
+            out[kind, 2, h] = (d, "x", step)
+    return out
+
+
+MESSAGES = {**plane_messages(), **line_messages()}
+
+
+PRIORITY = (
+    62, 23, 50, 16, 52, 27, 0, 32, 58, 39, 6, 33, 66, 43, 60, 68, 13, 7,
+    10, 56, 5, 49, 38, 18, 51, 54, 15, 1, 35, 46, 2, 55, 19, 29, 71, 44,
+    64, 53, 59, 8, 37, 28, 67, 63, 70, 45, 47, 69, 17, 65, 3, 14, 30, 9,
+    31, 36, 61, 4, 41, 11, 12, 48, 42, 22, 34, 40, 21, 24, 20, 25, 26, 57,
+)
 
 
 def make_schedule():
-    wire, hop, tile, local = 5.6, 2.2, 1.3, 1.4
-    messages = {**plane_messages(), **line_messages()}
-    free = {}
-    arrive = {}
+    wire, hop, tile, local = 2.8, 2.2, 1.4, 1.5
+    order = dict(zip(MESSAGES, PRIORITY))
+    free, arrive, waited, have = {}, {}, {}, {}
 
     def launch(name, when):
-        _, axis, step = messages[name]
-        begin = max(free.get((axis, step), 0.0), when)
-        free[axis, step] = begin + wire
-        arrive[name] = begin + wire + hop
-
-    def after(kind, slot):
-        return [n for n, m in messages.items() if n[0] == kind and m[0] == slot]
-
-    first = []
-    for kind, own in (("u", (0, 0)), ("v", (0, 0)), ("ku", 0), ("kv", 0)):
-        first += after(kind, own)
-    order = {n: i for i, n in enumerate(messages)}
-    first.sort(key=lambda n: order[n])
+        _, axis, step = MESSAGES[name]
+        free[axis, step] = max(free.get((axis, step), 0.0), when) + wire
+        arrive[name] = free[axis, step] + hop
+
+    def after(kind, slot, half):
+        found = [
+            n for n, m in MESSAGES.items() if n[0] == kind and m[0] == slot and n[2] == half
+        ]
+        return tuple(sorted(found, key=order.get))
+
+    own = (("u", (0, 0)), ("v", (0, 0)), ("ku", 0), ("kv", 0))
+    first = sorted((n for k in own for h in range(2) for n in after(*k, h)), key=order.get)
     for name in first:
         launch(name, 0.0)
-    now, waited, done_tiles = 0.0, {}, []
-    sequence = [("launch", tuple(first))]
-    pending_actions = []
-    steps = []
     slots = [(dy, dz) for dz in range(4) for dy in range(4)]
-    have = {("u", (0, 0)): 0.0, ("v", (0, 0)): 0.0}
-    while len(done_tiles) < 16:
-        coming = sorted((t, order[n], n) for n, t in arrive.items() if n not in waited)
-        keys_in = all(n in waited for n in line_messages())
-        ready = []
-        if keys_in:
-            ready = [
-                s
-                for s in slots
-                if s not in done_tiles
-                and all((k, s) in have and have[k, s] + local <= now for k in ("u", "v"))
-            ]
-        if coming and coming[0][0] <= now or (coming and not ready):
-            t, _, name = coming[0]
-            now = max(now, t) + 0.05
+    whole = {("u", (0, 0)): 0.0, ("v", (0, 0)): 0.0}
+    now, tiles, steps, actions = 0.0, [], [], []
+    lines = list(line_messages())
+
+    def ready_at(slot):
+        return max(whole.get((k, slot), 1e9) for k in ("u", "v")) + local
+
+    while len(tiles) < 16:
+        coming = min(((t, order[n], n) for n, t in arrive.items() if n not in waited), default=None)
+        able = [s for s in slots if s not in tiles and ready_at(s) <= now]
+        if not all(n in waited for n in lines):
+            able = []
+        if coming and (coming[0] <= now or not able):
+            now = max(now, coming[0]) + 0.05
+            name = coming[2]
             waited[name] = now
-            follow = after(name[0], name[1])
+            follow = after(*name)
             for f in follow:
                 launch(f, now)
-            if name[0] in ("u", "v"):
-                have[name] = now
-            pending_actions.append((name, tuple(follow)))
-        elif ready:
-            ready.sort(key=lambda s: (max(have["u", s], have["v", s]), slots.index(s)))
-            done_tiles.append(ready[0])
-            steps.append(tuple(pending_actions))
-            pending_actions = []
+            kind, slot, half = name
+            complete = (kind, slot, 1 - half) in waited
+            if complete:
+                whole[kind, slot] = now
+            actions.append((name, follow, complete and kind in ("u", "v")))
+        elif able:
+            best = min(able, key=lambda s: (ready_at(s), slots.index(s)))
+            tiles.append(best)
+            steps.append(tuple(actions))
+            actions = []
             now += tile
         else:
-            now = min(
-                max(have["u", s], have["v", s]) + local + 1e-6
-                for s in slots
-                if s not in done_tiles and ("u", s) in have and ("v", s) in have
-            )
-    return tuple(first), tuple(steps), tuple(done_tiles), now
+            now = min(ready_at(s) for s in slots if s not in tiles) + 1e-6
+    return tuple(first), tuple(steps), tuple(tiles), now
 
 
 FIRST, STEPS, TILES, _ = make_schedule()
 SLOT = {s: k for k, s in enumerate(TILES)}
-MESSAGES = {**plane_messages(), **line_messages()}
 NAMES = (
     list(MESSAGES)
     + [("pu", s) for s in TILES]
     + [("pv", s) for s in TILES]
-    + [(kind, d) for kind in ("lx", "ly", "lz", "sx", "sy", "sz", "ox") for d in RING]
+    + [(kind, d) for kind in ("lx", "sx", "ox") for d in RING]
+    + [(kind, o) for kind in ("l", "s") for o in OTHERS]
     + [("lp", 0), ("sp", 0)]
     + [("r", i) for i in range(6)]
 )
@@ -154,7 +162,8 @@
     key_coef,
     anchor_coef,
     loss_line,
-    gbuf,
+    gbuf0,
+    gbuf1,
     total,
     relay,
     arrive,
@@ -174,6 +183,9 @@
         if axis == "x":
             there = lax.rem(x + step + 4, 4)
             return {"x_hi": there // 2, "x_lo": lax.rem(there, 2)}
+        if axis == "plane":
+            dy, dz = step
+            return {"y": lax.rem(y + 4 - dy, 4), "z": lax.rem(z + 4 - dz, 4)}
         place = y if axis == "y" else z
         return {axis: lax.rem(place + step + 4, 4)}
 
@@ -185,16 +197,21 @@
 
     half = rows // 2
 
+    def part_of(start, h):
+        return pl.ds(start + h * half, half)
+
     def refs_of(name):
-        kind, slot = name
+        kind, slot = name[:2]
         if kind in ("u", "v"):
             source, axis, step = MESSAGES[name]
             buf = ua if kind == "u" else va
-            return buf.at[own_rows(source)], buf.at[own_rows(slot)], axis, step
+            here, there = SLOT[source] * pair, SLOT[slot] * pair
+            return buf.at[part_of(here, name[2])], buf.at[part_of(there, name[2])], axis, step
         if kind in ("ku", "kv"):
             source, axis, step = MESSAGES[name]
             buf = uk if kind == "ku" else vk
-            return buf.at[key_rows(source)], buf.at[key_rows(slot)], axis, step
+            here, there = KEY_POS[source] * rows, KEY_POS[slot] * rows
+            return buf.at[part_of(here, name[2])], buf.at[part_of(there, name[2])], axis, step
         if kind in ("pu", "pv"):
             buf = ua if kind == "pu" else va
             there = pl.ds(SLOT[slot] * pair + rows, rows)
@@ -205,10 +222,8 @@
         if kind == "sx":
             return part, part_in.at[slot - 1], "x", -slot
         plane = label_plane if kind[0] == "l" else coef_plane
-        if kind in ("ly", "sy"):
-            return plane.at[0, 0, 0], plane.at[0, 0, slot], "y", -slot
-        if kind in ("lz", "sz"):
-            return plane.at[0, 0], plane.at[0, slot], "z", -slot
+        if kind in ("l", "s"):
+            return plane.at[0, 0, 0], plane.at[0, slot[1], slot[0]], "plane", slot
         if kind in ("lp", "sp"):
             return plane.at[0], plane.at[1], "core", 0
         two, nxt, prv = KEY_POS[2] * rows, KEY_POS[1] * rows, KEY_POS[3] * rows
@@ -241,8 +256,8 @@
             message(name).wait_recv()
 
     barrier = pltpu.get_barrier_semaphore()
-    for axis in ("x", "y", "z"):
-        for d in RING:
+    for axis, steps in (("x", RING), ("plane", OTHERS)):
+        for d in steps:
             pl.semaphore_signal(barrier, inc=1, device_id=device(axis, d), device_id_type=MESH)
     pl.semaphore_signal(barrier, inc=1, device_id=device("core", 0), device_id_type=MESH)
 
@@ -264,23 +279,21 @@
     label_plane[0, 0, 0] = own_label
     label_line[0] = own_label
     acc[...] = jnp.zeros_like(acc)
-    pl.semaphore_wait(barrier, 10)
-
-    start(*[("ly", d) for d in RING], *[("lx", d) for d in RING])
+    total[...] = jnp.zeros_like(total)
+    pl.semaphore_wait(barrier, 19)
+
+    start(*[("l", o) for o in OTHERS], *[("lx", d) for d in RING])
     start(*FIRST)
     start(("pu", (0, 0)), ("pv", (0, 0)))
-    arrived(*[("ly", d) for d in RING])
-    start(*[("lz", d) for d in RING])
-    arrived(*[("lx", d) for d in RING])
-    for d in range(4):
-        line = label_line[d][0:1]
-        key_label[key_rows(d), :] = jnp.broadcast_to(line, (rows, rows)).T
-    arrived(*[("lz", d) for d in RING])
-    start(("lp", 0))
-    arrived(("lp", 0))
-    for (dy, dz), k in SLOT.items():
-        for c in range(2):
-            anchor_label[:, pl.ds(k * pair + c * rows, rows)] = label_plane[c, dz, dy]
+
+    def labels_in():
+        arrived(("lp", 0), *[("lx", d) for d in RING])
+        for d in range(4):
+            line = label_line[d][0:1]
+            key_label[key_rows(d), :] = jnp.broadcast_to(line, (rows, rows)).T
+        for (dy, dz), k in SLOT.items():
+            for c in range(2):
+                anchor_label[:, pl.ds(k * pair + c * rows, rows)] = label_plane[c, dz, dy]
 
     chunk = 32
     k_rel = LOG2E / temp_student
@@ -323,12 +336,17 @@
         for n, actions in enumerate(STEPS):
             @pl.when(k == n)
             def _(n=n, actions=actions):
-                for name, follow in actions:
+                for i, (name, follow, complete) in enumerate(actions):
+                    if n == 0 and i == 10:
+                        arrived(*[("l", o) for o in OTHERS])
+                        start(("lp", 0))
                     arrived(name)
                     start(*follow)
-                    if name[0] in ("u", "v"):
+                    if complete:
                         start(("p" + name[0], name[1]))
                 arrived(("pu", TILES[n]), ("pv", TILES[n]))
+                if n == 0:
+                    labels_in()
 
         here = pl.ds(pl.multiple_of(k * pair, pair), pair)
         raw_s[...] = lax.dot_general(uk[...], ua[here, :], contract, preferred_element_type=F32)
@@ -358,7 +376,8 @@
     start(*[("sx", d) for d in RING])
     arrived(*[("sx", d) for d in RING])
     line = lax.broadcasted_iota(jnp.int32, (8, rows), 0)
-    for e in range(4):
+
+    def coefficients(e):
         sums = part[e]
         for d in RING:
             sums = sums + part_in[d - 1, (e - d) % 4]
@@ -370,8 +389,6 @@
             (1.0 / temp_student) / tea,
             (1.0 / temp_sup) / positives,
         )
-        for n in range(4):
-            key_coef[n, key_rows(e), :] = jnp.broadcast_to(coefs[n], (rows, rows)).T
         if e == 0:
             contrast = (1.0 - sums[4:5] / positives) / temp_sup + jnp.log(sup)
             relation = (1.0 - sums[3:4] / tea) / temp_student + jnp.log(rel)
@@ -379,63 +396,76 @@
             for n, value in enumerate((*coefs, contrast, relation)):
                 mine = jnp.where(line == n, jnp.broadcast_to(value, (8, rows)), mine)
             coef_plane[0, 0, 0] = mine
-            start(*[("sy", d) for d in RING])
+            start(*[("s", o) for o in OTHERS])
+        for n in range(4):
+            key_coef[n, key_rows(e), :] = jnp.broadcast_to(coefs[n], (rows, rows)).T
 
     depth = 4 * rows
     chunks = 32 * rows // depth
 
-    def fill(c, first, count, side):
-        def one(i, carry):
-            r = pl.ds(pl.multiple_of(first + i * chunk, chunk), chunk)
-            g = pl.ds(pl.multiple_of(i * chunk, chunk), chunk)
+    def fill(c, first, count, sides, out):
+        for i in range(count // chunk):
+            r = pl.ds(first + i * chunk, chunk)
             for q in range(depth // rows):
                 columns = pl.ds(pl.multiple_of(c * depth + q * rows, rows), rows)
                 sb = signed_b[r, columns]
                 w = w_all[r, columns]
-                if side == "key":
-                    ca, cb, cw, cp = [key_coef[n, r, :] for n in range(4)]
-                else:
-                    ca, cb, cw, cp = [
-                        jnp.broadcast_to(anchor_coef[n : n + 1, columns], sb.shape)
-                        for n in range(4)
-                    ]
-                value = (sb * sb * ca - jnp.where(sb < 0.0, cp, 0.0)) + (
-                    jnp.abs(sb) * cb - w * cw
-                )
-                gbuf[g, pl.ds(q * rows, rows)] = value.astype(BF16)
+                b, a, positive = jnp.abs(sb), sb * sb, sb < 0.0
+                for n, side in enumerate(sides):
+                    if side == "key":
+                        ca, cb, cw, cp = [key_coef[m, r, :] for m in range(4)]
+                    else:
+                        ca, cb, cw, cp = [
+                            jnp.broadcast_to(anchor_coef[m : m + 1, columns], sb.shape)
+                            for m in range(4)
+                        ]
+                    value = (a * ca - jnp.where(positive, cp, 0.0)) + (b * cb - w * cw)
+                    out[pl.ds(n * count + i * chunk, chunk), pl.ds(q * rows, rows)] = value.astype(
+                        BF16
+                    )
+
+    def multiply(c, first, count, sides, out):
+        anchors = ua[pl.ds(pl.multiple_of(c * depth, depth), depth), :]
+        made = out[pl.ds(0, count * len(sides)), :]
+        product = jnp.dot(made, anchors, preferred_element_type=F32)
+        if len(sides) == 2:
+            product = product[0:count] + product[count : 2 * count]
+        total[pl.ds(first, count), :] += product
+
+    def second_pass(first, count, sides):
+        fill(0, first, count, sides, gbuf0)
+
+        def one(j, carry):
+            c = 2 * j
+            multiply(c, first, count, sides, gbuf0)
+            fill(c + 1, first, count, sides, gbuf1)
+            multiply(c + 1, first, count, sides, gbuf1)
+            fill(jnp.minimum(c + 2, chunks - 1), first, count, sides, gbuf0)
             return carry
 
-        lax.fori_loop(0, count // chunk, one, 0)
-
-    def multiply(c, first, count, fresh):
-        anchors = ua[pl.ds(pl.multiple_of(c * depth, depth), depth), :]
-        product = jnp.dot(gbuf[pl.ds(0, count), :], anchors, preferred_element_type=F32)
-        if fresh:
-            total[pl.ds(first, count), :] = product
-        else:
-            total[pl.ds(first, count), :] += product
-
-    def key_side(c, carry):
-        @pl.when(c == 2)
-        def _():
-            arrived(*[("sy", d) for d in RING])
-            start(*[("sz", d) for d in RING])
-
-        @pl.when(c == 5)
-        def _():
-            arrived(*[("sz", d) for d in RING])
-            start(("sp", 0))
-
-        fill(c, 0, key_count, "key")
-        multiply(c, 0, key_count, False)
-        return carry
-
-    total[...] = jnp.zeros_like(total)
-    lax.fori_loop(0, chunks, key_side, 0)
+        lax.fori_loop(0, chunks // 2, one, 0)
+
+    coefficients(0)
+    coefficients(2)
+    second_pass(0, rows, ("key",))
+    arrived(*[("s", o) for o in OTHERS])
+    start(("sp", 0))
+    coefficients(1)
+    coefficients(3)
     arrived(("sp", 0))
     for (dy, dz), k in SLOT.items():
         for c in range(2):
             anchor_coef[:, pl.ds(k * pair + c * rows, rows)] = coef_plane[c, dz, dy]
+    second_pass(0, rows, ("anchor",))
+    start(("r", 0), ("r", 1))
+    second_pass(rows, 2 * rows, ("key", "anchor"))
+    start(("r", 2), ("r", 3))
+    arrived(("r", 0))
+    total[pl.ds(KEY_POS[1] * rows, half), :] += relay[0]
+    start(("r", 4))
+    arrived(("r", 1))
+    total[pl.ds(KEY_POS[3] * rows + half, half), :] += relay[1]
+    start(("r", 5))
     losses = jnp.zeros((8, rows), F32)
     for cc in range(2):
         for zz in range(4):
@@ -445,26 +475,7 @@
                 ]
     loss_line[0] = losses
     start(*[("ox", d) for d in RING])
-
-    def anchor_side(first, count):
-        def one(c, carry):
-            fill(c, first, count, "anchor")
-            multiply(c, first, count, False)
-            return carry
-
-        lax.fori_loop(0, chunks, one, 0)
-
-    anchor_side(0, rows)
-    start(("r", 0), ("r", 1))
-    anchor_side(rows, 2 * rows)
-    start(("r", 2), ("r", 3))
-    arrived(("r", 0))
-    total[pl.ds(KEY_POS[1] * rows, half), :] += relay[0]
-    start(("r", 4))
-    arrived(("r", 1))
-    total[pl.ds(KEY_POS[3] * rows + half, half), :] += relay[1]
-    start(("r", 5))
-    anchor_side(own_key, rows)
+    second_pass(own_key, rows, ("key", "anchor"))
 
     arrived(*[("ox", d) for d in RING])
     sums = jnp.zeros((8, rows), F32)
@@ -524,6 +535,7 @@
             pltpu.VMEM((8, anchors), F32),
             pltpu.VMEM((4, 8, rows), F32),
             pltpu.VMEM((keys, 4 * rows), BF16),
+            pltpu.VMEM((keys, 4 * rows), BF16),
             pltpu.VMEM((keys, width), F32),
             pltpu.VMEM((2, rows // 2, width), F32),
             pltpu.VMEM((2, rows, width), F32),

time: 108 us -> 99.5 us (0.921)
  Pallas kernels: 104 us -> 95.5 us
    pallas_call x1, Pallas kernels: 104 us -> 95.5 us  [body(): pl.pallas_call(kernel, out_shape=(jax.ShapeDtypeStruct((rows, width), F32...]
where the time goes in v2:
time: 99.5 us; the launch traced here: 99.3 us
  Pallas kernels  95.5 us (96%)
  local copies, waits for them, and re-layouts  3.16 us (3%)
    pallas_call x1, Pallas kernels, body(): pl.pallas_call(kernel, out_shape=(jax.ShapeDtypeStruct((rows, width), F32...  95.5 us

profile of v2, /device:TPU:1, one launch (start us, length us, event | category | flops | bytes accessed | tf_op | source)
XLA Modules:
  0.0 99.3 jit_solution(10341475677715029397)
XLA Ops:
  0.6 95.5 %shard_map.58 = (f32[128,1024]{1,0:T(8,128)}, f32[8,128]{1,0:T(8,128)}) custom-call(bf16[128,1024]{1,0:T(8,128)(2,1)} %student_ref.1, bf16[128,1024]{1,0:T(8,128)(2,1)} %teacher_ref.1, s32[1,128]{1,0:T(1,128)} %bitcast.3), custom_call_target="tpu_custom_call" | custom-call | tf_op jit(solution)/shard_map/pallas_call | solution.py:509
  96.1 1.3 %fusion = (f32[1,1]{1,0:T(1,128)}, f32[1,1]{1,0:T(1,128)}) fusion(f32[8,128]{1,0:T(8,128)} %get-tuple-element.5), kind=kLoop, calls=%fused_computation | loop fusion | bytes 16 | tf_op jit(solution)/shard_map/slice | solution.py:549
  97.4 1.9 %copy.7 = f32[128,1024]{1,0:T(8,128)} copy(f32[128,1024]{1,0:T(8,128)} %get-tuple-element.14) | data formatting | bytes 1048576

commit v3 on v2

--- a/solution.py
+++ b/solution.py
@@ -20,7 +20,7 @@
 
 KEY_POS = {2: 0, 1: 1, 3: 2, 0: 3}
 RING = (1, 2, 3)
-OTHERS = [(dy, dz) for dz in range(4) for dy in range(4) if (dy, dz) != (0, 0)]
+OTHERS = [(dy, dz, c) for c in range(2) for dz in range(4) for dy in range(4)][1:]
 
 
 def plane_messages():
@@ -124,22 +124,27 @@
 
 
 FIRST, STEPS, TILES, _ = make_schedule()
+LATER = tuple(
+    n
+    for n in FIRST
+    if MESSAGES[n][1] == "z" and n != next(m for m in FIRST if MESSAGES[m][1:] == MESSAGES[n][1:])
+)
 SLOT = {s: k for k, s in enumerate(TILES)}
 NAMES = (
     list(MESSAGES)
     + [("pu", s) for s in TILES]
     + [("pv", s) for s in TILES]
-    + [(kind, d) for kind in ("lx", "sx", "ox") for d in RING]
-    + [(kind, o) for kind in ("l", "s") for o in OTHERS]
-    + [("lp", 0), ("sp", 0)]
+    + [(kind, d) for kind in ("lx", "ly", "lz", "sx", "ox") for d in RING]
+    + [("s", o) for o in OTHERS]
+    + [("lp", 0)]
     + [("r", i) for i in range(6)]
 )
 IDS = {n: i for i, n in enumerate(NAMES)}
 
 
 def kernel(
-    student_ref,
-    teacher_ref,
+    student_hbm,
+    teacher_hbm,
     label_ref,
     grad_ref,
     loss_ref,
@@ -167,8 +172,11 @@
     total,
     relay,
     arrive,
+    student_ref,
+    teacher_ref,
     send_sem,
     recv_sem,
+    load_sem,
 ):
     rows, width = student_ref.shape
     x_lo, x_hi = lax.axis_index("x_lo"), lax.axis_index("x_hi")
@@ -184,8 +192,9 @@
             there = lax.rem(x + step + 4, 4)
             return {"x_hi": there // 2, "x_lo": lax.rem(there, 2)}
         if axis == "plane":
-            dy, dz = step
-            return {"y": lax.rem(y + 4 - dy, 4), "z": lax.rem(z + 4 - dz, 4)}
+            dy, dz, c = step
+            there = {"y": lax.rem(y + 4 - dy, 4), "z": lax.rem(z + 4 - dz, 4)}
+            return {**there, "core": 1 - core if c else core}
         place = y if axis == "y" else z
         return {axis: lax.rem(place + step + 4, 4)}
 
@@ -221,11 +230,15 @@
             return buf.at[0], buf.at[slot], "x", -slot
         if kind == "sx":
             return part, part_in.at[slot - 1], "x", -slot
-        plane = label_plane if kind[0] == "l" else coef_plane
-        if kind in ("l", "s"):
-            return plane.at[0, 0, 0], plane.at[0, slot[1], slot[0]], "plane", slot
-        if kind in ("lp", "sp"):
-            return plane.at[0], plane.at[1], "core", 0
+        if kind == "s":
+            dy, dz, c = slot
+            return coef_plane.at[0, 0, 0], coef_plane.at[c, dz, dy], "plane", slot
+        if kind == "ly":
+            return label_plane.at[0, 0, 0], label_plane.at[0, 0, slot], "y", -slot
+        if kind == "lz":
+            return label_plane.at[0, 0], label_plane.at[0, slot], "z", -slot
+        if kind == "lp":
+            return label_plane.at[0], label_plane.at[1], "core", 0
         two, nxt, prv = KEY_POS[2] * rows, KEY_POS[1] * rows, KEY_POS[3] * rows
         return (
             (total.at[pl.ds(two, half)], relay.at[0], "x", 1),
@@ -255,12 +268,21 @@
         for name in names:
             message(name).wait_recv()
 
+    loads = [
+        pltpu.make_async_copy(student_hbm, student_ref, load_sem.at[0]),
+        pltpu.make_async_copy(teacher_hbm, teacher_ref, load_sem.at[1]),
+    ]
+    for load in loads:
+        load.start()
+
     barrier = pltpu.get_barrier_semaphore()
-    for axis, steps in (("x", RING), ("plane", OTHERS)):
-        for d in steps:
+    for axis in ("x", "y", "z"):
+        for d in RING:
             pl.semaphore_signal(barrier, inc=1, device_id=device(axis, d), device_id_type=MESH)
     pl.semaphore_signal(barrier, inc=1, device_id=device("core", 0), device_id_type=MESH)
 
+    for load in loads:
+        load.wait()
     own_key = KEY_POS[0] * rows
 
     def normalise(i, carry):
@@ -280,11 +302,14 @@
     label_line[0] = own_label
     acc[...] = jnp.zeros_like(acc)
     total[...] = jnp.zeros_like(total)
-    pl.semaphore_wait(barrier, 19)
-
-    start(*[("l", o) for o in OTHERS], *[("lx", d) for d in RING])
-    start(*FIRST)
+    pl.semaphore_wait(barrier, 10)
+
+    start(*[("ly", d) for d in RING], *[("lx", d) for d in RING])
+    start(*[name for name in FIRST if name not in LATER])
     start(("pu", (0, 0)), ("pv", (0, 0)))
+    arrived(*[("ly", d) for d in RING])
+    start(*[("lz", d) for d in RING])
+    start(*LATER)
 
     def labels_in():
         arrived(("lp", 0), *[("lx", d) for d in RING])
@@ -337,8 +362,8 @@
             @pl.when(k == n)
             def _(n=n, actions=actions):
                 for i, (name, follow, complete) in enumerate(actions):
-                    if n == 0 and i == 10:
-                        arrived(*[("l", o) for o in OTHERS])
+                    if n == 0 and i == 8:
+                        arrived(*[("lz", d) for d in RING])
                         start(("lp", 0))
                     arrived(name)
                     start(*follow)
@@ -403,9 +428,11 @@
     depth = 4 * rows
     chunks = 32 * rows // depth
 
-    def fill(c, first, count, sides, out):
-        for i in range(count // chunk):
-            r = pl.ds(first + i * chunk, chunk)
+    def fill(c, ranges, sides, out):
+        size = sum(count for _, count in ranges)
+        blocks = [f + i for f, count in ranges for i in range(0, count, chunk)]
+        for i, first in enumerate(blocks):
+            r = pl.ds(first, chunk)
             for q in range(depth // rows):
                 columns = pl.ds(pl.multiple_of(c * depth + q * rows, rows), rows)
                 sb = signed_b[r, columns]
@@ -420,46 +447,62 @@
                             for m in range(4)
                         ]
                     value = (a * ca - jnp.where(positive, cp, 0.0)) + (b * cb - w * cw)
-                    out[pl.ds(n * count + i * chunk, chunk), pl.ds(q * rows, rows)] = value.astype(
-                        BF16
-                    )
-
-    def multiply(c, first, count, sides, out):
+                    there = pl.ds(n * size + i * chunk, chunk)
+                    out[there, pl.ds(q * rows, rows)] = value.astype(BF16)
+
+    def multiply(c, ranges, sides, out):
+        size = sum(count for _, count in ranges)
         anchors = ua[pl.ds(pl.multiple_of(c * depth, depth), depth), :]
-        made = out[pl.ds(0, count * len(sides)), :]
+        made = out[pl.ds(0, size * len(sides)), :]
         product = jnp.dot(made, anchors, preferred_element_type=F32)
         if len(sides) == 2:
-            product = product[0:count] + product[count : 2 * count]
-        total[pl.ds(first, count), :] += product
-
-    def second_pass(first, count, sides):
-        fill(0, first, count, sides, gbuf0)
+            product = product[0:size] + product[size : 2 * size]
+        at = 0
+        for first, count in ranges:
+            total[pl.ds(first, count), :] += product[at : at + count]
+            at += count
+
+    def coefficients_in(c):
+        for k in range(c * depth // pair, (c + 1) * depth // pair):
+            dy, dz = TILES[k]
+            for side in range(2):
+                if (dy, dz, side) != (0, 0, 0):
+                    arrived(("s", (dy, dz, side)))
+                anchor_coef[:, pl.ds(k * pair + side * rows, rows)] = coef_plane[side, dz, dy]
+
+    def second_pass(ranges, sides, staged=False):
+        if staged:
+            coefficients_in(0)
+        fill(0, ranges, sides, gbuf0)
 
         def one(j, carry):
             c = 2 * j
-            multiply(c, first, count, sides, gbuf0)
-            fill(c + 1, first, count, sides, gbuf1)
-            multiply(c + 1, first, count, sides, gbuf1)
-            fill(jnp.minimum(c + 2, chunks - 1), first, count, sides, gbuf0)
+            if staged:
+                for n in range(chunks // 2):
+                    @pl.when(j == n)
+                    def _(n=n):
+                        for piece in range(2 * n + 1, min(2 * n + 3, chunks)):
+                            coefficients_in(piece)
+
+            multiply(c, ranges, sides, gbuf0)
+            fill(c + 1, ranges, sides, gbuf1)
+            multiply(c + 1, ranges, sides, gbuf1)
+            fill(jnp.minimum(c + 2, chunks - 1), ranges, sides, gbuf0)
             return carry
 
         lax.fori_loop(0, chunks // 2, one, 0)
 
+    both = ("key", "anchor")
     coefficients(0)
     coefficients(2)
-    second_pass(0, rows, ("key",))
-    arrived(*[("s", o) for o in OTHERS])
-    start(("sp", 0))
+    second_pass([(0, rows)], ("key",))
     coefficients(1)
     coefficients(3)
-    arrived(("sp", 0))
-    for (dy, dz), k in SLOT.items():
-        for c in range(2):
-            anchor_coef[:, pl.ds(k * pair + c * rows, rows)] = coef_plane[c, dz, dy]
-    second_pass(0, rows, ("anchor",))
+    second_pass([(0, rows)], ("anchor",), staged=True)
     start(("r", 0), ("r", 1))
-    second_pass(rows, 2 * rows, ("key", "anchor"))
+    second_pass([(KEY_POS[1] * rows + half, rows)], both)
     start(("r", 2), ("r", 3))
+    second_pass([(KEY_POS[1] * rows, half), (KEY_POS[3] * rows + half, half)], both)
     arrived(("r", 0))
     total[pl.ds(KEY_POS[1] * rows, half), :] += relay[0]
     start(("r", 4))
@@ -475,7 +518,7 @@
                 ]
     loss_line[0] = losses
     start(*[("ox", d) for d in RING])
-    second_pass(own_key, rows, ("key", "anchor"))
+    second_pass([(own_key, rows)], both)
 
     arrived(*[("ox", d) for d in RING])
     sums = jnp.zeros((8, rows), F32)
@@ -489,30 +532,42 @@
     def finish(i, carry):
         here = pl.ds(pl.multiple_of(i * 16, 16), 16)
         there = pl.ds(pl.multiple_of(own_key + i * 16, 16), 16)
+        grad_ref[here, :] = total[there, :] + arrive[0, here, :] + arrive[1, here, :]
+        return carry
+
+    lax.fori_loop(0, rows // 16, finish, 0)
+    for name in NAMES:
+        message(name).wait_send()
+
+
+def project(student_ref, sum_ref, loss_in_ref, grad_ref, supcon_ref, relation_ref):
+    def one(i, carry):
+        here = pl.ds(pl.multiple_of(i * 16, 16), 16)
         values = student_ref[here, :].astype(F32)
         scaling = lax.rsqrt(jnp.sum(values * values, axis=1, keepdims=True) + epsilon)
         unit = values * scaling
-        grad = total[there, :] + arrive[0, here, :] + arrive[1, here, :]
+        grad = sum_ref[here, :]
         along = jnp.sum(unit * grad, axis=1, keepdims=True)
         grad_ref[here, :] = scaling * (grad - unit * along)
         return carry
 
-    lax.fori_loop(0, rows // 16, finish, 0)
-    for name in NAMES:
-        message(name).wait_send()
+    lax.fori_loop(0, student_ref.shape[0] // 16, one, 0)
+    supcon_ref[0, 0] = loss_in_ref[4, 0]
+    relation_ref[0, 0] = loss_in_ref[5, 0]
 
 
 def body(student, teacher, labels):
     rows, width = student.shape
     keys, anchors = 4 * rows, 32 * rows
     vmem = pl.BlockSpec(memory_space=pltpu.VMEM)
-    grad, losses = pl.pallas_call(
+    hbm = pl.BlockSpec(memory_space=pltpu.HBM)
+    sums, losses = pl.pallas_call(
         kernel,
         out_shape=(
             jax.ShapeDtypeStruct((rows, width), F32),
             jax.ShapeDtypeStruct((8, rows), F32),
         ),
-        in_specs=[vmem] * 3,
+        in_specs=[hbm, hbm, vmem],
         out_specs=(vmem, vmem),
         scratch_shapes=[
             pltpu.VMEM((anchors, width), BF16),
@@ -539,14 +594,25 @@
             pltpu.VMEM((keys, width), F32),
             pltpu.VMEM((2, rows // 2, width), F32),
             pltpu.VMEM((2, rows, width), F32),
+            pltpu.VMEM((rows, width), BF16),
+            pltpu.VMEM((rows, width), BF16),
             pltpu.SemaphoreType.DMA((len(NAMES),)),
             pltpu.SemaphoreType.DMA((len(NAMES),)),
+            pltpu.SemaphoreType.DMA((2,)),
         ],
         compiler_params=pltpu.CompilerParams(
             collective_id=0, has_side_effects=True, vmem_limit_bytes=60 * 1024 * 1024
         ),
     )(student, teacher, labels.reshape(1, rows))
-    return losses[4, 0], losses[5, 0], grad
+    smem = pl.BlockSpec(memory_space=pltpu.SMEM)
+    scalar = jax.ShapeDtypeStruct((1, 1), F32)
+    grad, supcon, relation = pl.pallas_call(
+        project,
+        out_shape=(jax.ShapeDtypeStruct((rows, width), F32), scalar, scalar),
+        in_specs=[vmem, vmem, smem],
+        out_specs=(vmem, smem, smem),
+    )(student, sums, losses)
+    return supcon.reshape(()), relation.reshape(()), grad
 
 
 def solution(mesh):

time: 99.5 us -> 95.1 us (0.956)
  local copies, waits for them, and re-layouts: 3.16 us -> 0 us
  Pallas kernels: 95.5 us -> 94.3 us
    pallas_call x1, Pallas kernels: 95.5 us -> 90.9 us  [body(): pl.pallas_call(kernel, out_shape=(jax.ShapeDtypeStruct((rows, width), F32...]
    pallas_call x0 -> x1, Pallas kernels: none -> 3.42 us  [body(): pl.pallas_call(project, out_shape=(jax.ShapeDtypeStruct((rows, width), F3...]
    unnamed x1 -> x0, local copies, waits for them, and re-layouts: 1.88 us -> none
    slice x1 -> x0, local copies, waits for them, and re-layouts: 1.28 us -> none  [body(): return (losses[4, 0], losses[5, 0], grad)]
where the time goes in v3:
time: 95.1 us; the launch traced here: 95 us
  Pallas kernels  94.3 us (99%)
    pallas_call x1, Pallas kernels, body(): pl.pallas_call(kernel, out_shape=(jax.ShapeDtypeStruct((rows, width), F32...  90.9 us
    pallas_call x1, Pallas kernels, body(): pl.pallas_call(project, out_shape=(jax.ShapeDtypeStruct((rows, width), F3...  3.42 us

profile of v3, /device:TPU:1, one launch (start us, length us, event | category | flops | bytes accessed | tf_op | source)
XLA Modules:
  0.0 95.0 jit_solution(8911957176251008198)
XLA Ops:
  0.6 90.9 %shard_map.58 = (f32[128,1024]{1,0:T(8,128)}, f32[8,128]{1,0:T(8,128)}) custom-call(bf16[128,1024]{1,0:T(8,128)(2,1)} %student_ref.1, bf16[128,1024]{1,0:T(8,128)(2,1)} %teacher_hbm.1, s32[1,128]{1,0:T(1,128)} %bitcast.3), custom_call_target="tpu_custom_call" | custom-call | tf_op jit(solution)/shard_map/pallas_call | solution.py:564
  91.6 3.4 %shard_map.59 = (f32[128,1024]{1,0:T(8,128)}, f32[1,1]{1,0:T(1,128)}, f32[1,1]{1,0:T(1,128)}) custom-call(bf16[128,1024]{1,0:T(8,128)(2,1)} %student_ref.1, f32[128,1024]{1,0:T(8,128)} %get-tuple-element.8.sum_ref, f32[8,128]{1,0:T(8,128)} %get-tuple-element.9.loss_in_ref), custom_call_target="tpu_custom_call" | custom-call | tf_op jit(solution)/shard_map/pallas_call | solution.py:609

commit v4 on v3

--- a/solution.py
+++ b/solution.py
@@ -60,15 +60,15 @@
 
 
 PRIORITY = (
-    62, 23, 50, 16, 52, 27, 0, 32, 58, 39, 6, 33, 66, 43, 60, 68, 13, 7,
-    10, 56, 5, 49, 38, 18, 51, 54, 15, 1, 35, 46, 2, 55, 19, 29, 71, 44,
-    64, 53, 59, 8, 37, 28, 67, 63, 70, 45, 47, 69, 17, 65, 3, 14, 30, 9,
-    31, 36, 61, 4, 41, 11, 12, 48, 42, 22, 34, 40, 21, 24, 20, 25, 26, 57,
+    62, 68, 46, 70, 12, 11, 71, 48, 31, 66, 13, 5, 35, 34, 4, 16, 19, 41,
+    22, 25, 49, 54, 42, 32, 37, 6, 67, 56, 21, 40, 47, 55, 30, 8, 0, 63,
+    61, 10, 24, 3, 1, 60, 18, 50, 28, 14, 2, 51, 29, 52, 64, 69, 17, 65,
+    9, 53, 7, 43, 26, 20, 36, 23, 58, 38, 39, 44, 27, 45, 59, 33, 57, 15,
 )
 
 
 def make_schedule():
-    wire, hop, tile, local = 2.8, 2.2, 1.4, 1.5
+    wire, hop, tile, local = 2.82, 3.4, 1.3, 2.0
     order = dict(zip(MESSAGES, PRIORITY))
     free, arrive, waited, have = {}, {}, {}, {}
 
@@ -146,7 +146,7 @@
     student_hbm,
     teacher_hbm,
     label_ref,
-    grad_ref,
+    sum_hbm,
     loss_ref,
     ua,
     va,
@@ -296,17 +296,17 @@
             keys[there, :] = unit
         return carry
 
-    lax.fori_loop(0, rows // 16, normalise, 0)
+    lax.fori_loop(0, rows // 16, normalise, 0, unroll=4)
     own_label = jnp.broadcast_to(label_ref[...].astype(F32), (8, rows))
     label_plane[0, 0, 0] = own_label
     label_line[0] = own_label
-    acc[...] = jnp.zeros_like(acc)
-    total[...] = jnp.zeros_like(total)
     pl.semaphore_wait(barrier, 10)
 
     start(*[("ly", d) for d in RING], *[("lx", d) for d in RING])
     start(*[name for name in FIRST if name not in LATER])
     start(("pu", (0, 0)), ("pv", (0, 0)))
+    acc[...] = jnp.zeros_like(acc)
+    total[...] = jnp.zeros_like(total)
     arrived(*[("ly", d) for d in RING])
     start(*[("lz", d) for d in RING])
     start(*LATER)
@@ -529,31 +529,73 @@
 
     arrived(("r", 2), ("r", 3), ("r", 4), ("r", 5))
 
-    def finish(i, carry):
-        here = pl.ds(pl.multiple_of(i * 16, 16), 16)
-        there = pl.ds(pl.multiple_of(own_key + i * 16, 16), 16)
-        grad_ref[here, :] = total[there, :] + arrive[0, here, :] + arrive[1, here, :]
-        return carry
-
-    lax.fori_loop(0, rows // 16, finish, 0)
+    piece = rows // 4
+    stores = []
+    for i in range(4):
+        here = pl.ds(i * piece, piece)
+        mine = pl.ds(own_key + i * piece, piece)
+        total[mine, :] += arrive[0, here, :] + arrive[1, here, :]
+        store = pltpu.make_async_copy(total.at[mine], sum_hbm.at[here], load_sem.at[2 + i])
+        store.start()
+        stores.append(store)
+    for store in stores:
+        store.wait()
     for name in NAMES:
         message(name).wait_send()
 
 
-def project(student_ref, sum_ref, loss_in_ref, grad_ref, supcon_ref, relation_ref):
-    def one(i, carry):
-        here = pl.ds(pl.multiple_of(i * 16, 16), 16)
-        values = student_ref[here, :].astype(F32)
-        scaling = lax.rsqrt(jnp.sum(values * values, axis=1, keepdims=True) + epsilon)
-        unit = values * scaling
-        grad = sum_ref[here, :]
-        along = jnp.sum(unit * grad, axis=1, keepdims=True)
-        grad_ref[here, :] = scaling * (grad - unit * along)
-        return carry
-
-    lax.fori_loop(0, student_ref.shape[0] // 16, one, 0)
-    supcon_ref[0, 0] = loss_in_ref[4, 0]
-    relation_ref[0, 0] = loss_in_ref[5, 0]
+def project(
+    student_hbm,
+    sum_hbm,
+    loss_hbm,
+    grad_hbm,
+    supcon_ref,
+    relation_ref,
+    student_ref,
+    sum_ref,
+    loss_ref,
+    grad_ref,
+    load_sem,
+    store_sem,
+):
+    rows = student_ref.shape[0]
+    piece = 32
+    pieces = [pl.ds(i, piece) for i in range(0, rows, piece)]
+    loads = []
+    for i, here in enumerate(pieces):
+        loads.append(
+            (
+                pltpu.make_async_copy(sum_hbm.at[here], sum_ref.at[here], load_sem.at[0, i]),
+                pltpu.make_async_copy(
+                    student_hbm.at[here], student_ref.at[here], load_sem.at[1, i]
+                ),
+            )
+        )
+    loss_load = pltpu.make_async_copy(loss_hbm, loss_ref, load_sem.at[2, 0])
+    for pair in loads:
+        for load in pair:
+            load.start()
+    loss_load.start()
+    stores = []
+    for i, here in enumerate(pieces):
+        for load in loads[i]:
+            load.wait()
+        for r in range(0, piece, 16):
+            part = pl.ds(i * piece + r, 16)
+            values = student_ref[part, :].astype(F32)
+            scaling = lax.rsqrt(jnp.sum(values * values, axis=1, keepdims=True) + epsilon)
+            unit = values * scaling
+            grad = sum_ref[part, :]
+            along = jnp.sum(unit * grad, axis=1, keepdims=True)
+            grad_ref[part, :] = scaling * (grad - unit * along)
+        store = pltpu.make_async_copy(grad_ref.at[here], grad_hbm.at[here], store_sem.at[i])
+        store.start()
+        stores.append(store)
+    loss_load.wait()
+    supcon_ref[0, 0] = loss_ref[4, 0]
+    relation_ref[0, 0] = loss_ref[5, 0]
+    for store in stores:
+        store.wait()
 
 
 def body(student, teacher, labels):
@@ -568,7 +610,7 @@
             jax.ShapeDtypeStruct((8, rows), F32),
         ),
         in_specs=[hbm, hbm, vmem],
-        out_specs=(vmem, vmem),
+        out_specs=(hbm, vmem),
         scratch_shapes=[
             pltpu.VMEM((anchors, width), BF16),
             pltpu.VMEM((anchors, width), BF16),
@@ -598,7 +640,7 @@
             pltpu.VMEM((rows, width), BF16),
             pltpu.SemaphoreType.DMA((len(NAMES),)),
             pltpu.SemaphoreType.DMA((len(NAMES),)),
-            pltpu.SemaphoreType.DMA((2,)),
+            pltpu.SemaphoreType.DMA((6,)),
         ],
         compiler_params=pltpu.CompilerParams(
             collective_id=0, has_side_effects=True, vmem_limit_bytes=60 * 1024 * 1024
@@ -609,8 +651,16 @@
     grad, supcon, relation = pl.pallas_call(
         project,
         out_shape=(jax.ShapeDtypeStruct((rows, width), F32), scalar, scalar),
-        in_specs=[vmem, vmem, smem],
-        out_specs=(vmem, smem, smem),
+        in_specs=[hbm, hbm, hbm],
+        out_specs=(hbm, smem, smem),
+        scratch_shapes=[
+            pltpu.VMEM((rows, width), BF16),
+            pltpu.VMEM((rows, width), F32),
+            pltpu.SMEM((8, rows), F32),
+            pltpu.VMEM((rows, width), F32),
+            pltpu.SemaphoreType.DMA((3, rows // 32)),
+            pltpu.SemaphoreType.DMA((rows // 32,)),
+        ],
     )(student, sums, losses)
     return supcon.reshape(()), relation.reshape(()), grad
 

time: 95.1 us -> 95.5 us (level)
  no operation moved by 1% of the time
where the time goes in v4:
time: 95.5 us; the launch traced here: 95.3 us
  Pallas kernels  94.7 us (99%)
    pallas_call x1, Pallas kernels, body(): pl.pallas_call(kernel, out_shape=(jax.ShapeDtypeStruct((rows, width), F32...  91.7 us
    pallas_call x1, Pallas kernels, body(): pl.pallas_call(project, out_shape=(jax.ShapeDtypeStruct((rows, width), F3...  3.01 us

profile of v4, /device:TPU:1, one launch (start us, length us, event | category | flops | bytes accessed | tf_op | source)
XLA Modules:
  0.0 95.3 jit_solution(17006983671721248985)
XLA Ops:
  0.6 91.7 %shard_map.58 = (f32[128,1024]{1,0:T(8,128)}, f32[8,128]{1,0:T(8,128)}) custom-call(bf16[128,1024]{1,0:T(8,128)(2,1)} %student_hbm.3, bf16[128,1024]{1,0:T(8,128)(2,1)} %teacher_hbm.1, s32[1,128]{1,0:T(1,128)} %bitcast.3), custom_call_target="tpu_custom_call" | custom-call | tf_op jit(solution)/shard_map/pallas_call | solution.py:606
  92.3 3.0 %shard_map.59 = (f32[128,1024]{1,0:T(8,128)}, f32[1,1]{1,0:T(1,128)}, f32[1,1]{1,0:T(1,128)}) custom-call(bf16[128,1024]{1,0:T(8,128)(2,1)} %student_hbm.3, f32[128,1024]{1,0:T(8,128)} %get-tuple-element.8.sum_hbm, f32[8,128]{1,0:T(8,128)} %get-tuple-element.9.loss_hbm), custom_call_target="tpu_custom_call" | custom-call | tf_op jit(solution)/shard_map/pallas_call | solution.py:651

commit v5 on v4

--- a/solution.py
+++ b/solution.py
@@ -146,7 +146,7 @@
     student_hbm,
     teacher_hbm,
     label_ref,
-    sum_hbm,
+    grad_ref,
     loss_ref,
     ua,
     va,
@@ -352,7 +352,7 @@
                 acc[n, r, :] += sums[n]
             return carry
 
-        lax.fori_loop(0, count // chunk, one, 0)
+        lax.fori_loop(0, count // chunk, one, 0, unroll=2)
 
     key_count = 4 * rows
     contract = (((1,), (1,)), ((), ()))
@@ -529,17 +529,13 @@
 
     arrived(("r", 2), ("r", 3), ("r", 4), ("r", 5))
 
-    piece = rows // 4
-    stores = []
-    for i in range(4):
-        here = pl.ds(i * piece, piece)
-        mine = pl.ds(own_key + i * piece, piece)
-        total[mine, :] += arrive[0, here, :] + arrive[1, here, :]
-        store = pltpu.make_async_copy(total.at[mine], sum_hbm.at[here], load_sem.at[2 + i])
-        store.start()
-        stores.append(store)
-    for store in stores:
-        store.wait()
+    def finish(i, carry):
+        here = pl.ds(pl.multiple_of(i * 16, 16), 16)
+        there = pl.ds(pl.multiple_of(own_key + i * 16, 16), 16)
+        grad_ref[here, :] = total[there, :] + arrive[0, here, :] + arrive[1, here, :]
+        return carry
+
+    lax.fori_loop(0, rows // 16, finish, 0)
     for name in NAMES:
         message(name).wait_send()
 
@@ -610,7 +606,7 @@
             jax.ShapeDtypeStruct((8, rows), F32),
         ),
         in_specs=[hbm, hbm, vmem],
-        out_specs=(hbm, vmem),
+        out_specs=(vmem, vmem),
         scratch_shapes=[
             pltpu.VMEM((anchors, width), BF16),
             pltpu.VMEM((anchors, width), BF16),
@@ -640,7 +636,7 @@
             pltpu.VMEM((rows, width), BF16),
             pltpu.SemaphoreType.DMA((len(NAMES),)),
             pltpu.SemaphoreType.DMA((len(NAMES),)),
-            pltpu.SemaphoreType.DMA((6,)),
+            pltpu.SemaphoreType.DMA((2,)),
         ],
         compiler_params=pltpu.CompilerParams(
             collective_id=0, has_side_effects=True, vmem_limit_bytes=60 * 1024 * 1024

time: 95.5 us -> 94.8 us (level)
  no operation moved by 1% of the time
where the time goes in v5:
time: 94.8 us; the launch traced here: 94.7 us
  Pallas kernels  94 us (99%)
    pallas_call x1, Pallas kernels, body(): pl.pallas_call(kernel, out_shape=(jax.ShapeDtypeStruct((rows, width), F32...  91 us
    pallas_call x1, Pallas kernels, body(): pl.pallas_call(project, out_shape=(jax.ShapeDtypeStruct((rows, width), F3...  3.01 us

profile of v5, /device:TPU:1, one launch (start us, length us, event | category | flops | bytes accessed | tf_op | source)
XLA Modules:
  0.0 94.7 jit_solution(3875593532954673935)
XLA Ops:
  0.6 91.0 %shard_map.58 = (f32[128,1024]{1,0:T(8,128)}, f32[8,128]{1,0:T(8,128)}) custom-call(bf16[128,1024]{1,0:T(8,128)(2,1)} %student_hbm.3, bf16[128,1024]{1,0:T(8,128)(2,1)} %teacher_hbm.1, s32[1,128]{1,0:T(1,128)} %bitcast.3), custom_call_target="tpu_custom_call" | custom-call | tf_op jit(solution)/shard_map/pallas_call | solution.py:602
  91.7 3.0 %shard_map.59 = (f32[128,1024]{1,0:T(8,128)}, f32[1,1]{1,0:T(1,128)}, f32[1,1]{1,0:T(1,128)}) custom-call(bf16[128,1024]{1,0:T(8,128)(2,1)} %student_hbm.3, f32[128,1024]{1,0:T(8,128)} %get-tuple-element.8.sum_hbm, f32[8,128]{1,0:T(8,128)} %get-tuple-element.9.loss_hbm), custom_call_target="tpu_custom_call" | custom-call | tf_op jit(solution)/shard_map/pallas_call | solution.py:647

commit v6 on v3

--- a/solution.py
+++ b/solution.py
@@ -60,15 +60,15 @@
 
 
 PRIORITY = (
-    62, 23, 50, 16, 52, 27, 0, 32, 58, 39, 6, 33, 66, 43, 60, 68, 13, 7,
-    10, 56, 5, 49, 38, 18, 51, 54, 15, 1, 35, 46, 2, 55, 19, 29, 71, 44,
-    64, 53, 59, 8, 37, 28, 67, 63, 70, 45, 47, 69, 17, 65, 3, 14, 30, 9,
-    31, 36, 61, 4, 41, 11, 12, 48, 42, 22, 34, 40, 21, 24, 20, 25, 26, 57,
+    62, 68, 46, 70, 12, 11, 71, 48, 31, 66, 13, 5, 35, 34, 4, 16, 19, 41,
+    22, 25, 49, 54, 42, 32, 37, 6, 67, 56, 21, 40, 47, 55, 30, 8, 0, 63,
+    61, 10, 24, 3, 1, 60, 18, 50, 28, 14, 2, 51, 29, 52, 64, 69, 17, 65,
+    9, 53, 7, 43, 26, 20, 36, 23, 58, 38, 39, 44, 27, 45, 59, 33, 57, 15,
 )
 
 
 def make_schedule():
-    wire, hop, tile, local = 2.8, 2.2, 1.4, 1.5
+    wire, hop, tile, local = 2.82, 3.4, 1.3, 2.0
     order = dict(zip(MESSAGES, PRIORITY))
     free, arrive, waited, have = {}, {}, {}, {}
 
@@ -296,17 +296,17 @@
             keys[there, :] = unit
         return carry
 
-    lax.fori_loop(0, rows // 16, normalise, 0)
+    lax.fori_loop(0, rows // 16, normalise, 0, unroll=4)
     own_label = jnp.broadcast_to(label_ref[...].astype(F32), (8, rows))
     label_plane[0, 0, 0] = own_label
     label_line[0] = own_label
-    acc[...] = jnp.zeros_like(acc)
-    total[...] = jnp.zeros_like(total)
     pl.semaphore_wait(barrier, 10)
 
     start(*[("ly", d) for d in RING], *[("lx", d) for d in RING])
     start(*[name for name in FIRST if name not in LATER])
     start(("pu", (0, 0)), ("pv", (0, 0)))
+    acc[...] = jnp.zeros_like(acc)
+    total[...] = jnp.zeros_like(total)
     arrived(*[("ly", d) for d in RING])
     start(*[("lz", d) for d in RING])
     start(*LATER)
@@ -352,7 +352,7 @@
                 acc[n, r, :] += sums[n]
             return carry
 
-        lax.fori_loop(0, count // chunk, one, 0)
+        lax.fori_loop(0, count // chunk, one, 0, unroll=2)
 
     key_count = 4 * rows
     contract = (((1,), (1,)), ((), ()))
@@ -532,28 +532,40 @@
     def finish(i, carry):
         here = pl.ds(pl.multiple_of(i * 16, 16), 16)
         there = pl.ds(pl.multiple_of(own_key + i * 16, 16), 16)
-        grad_ref[here, :] = total[there, :] + arrive[0, here, :] + arrive[1, here, :]
-        return carry
-
-    lax.fori_loop(0, rows // 16, finish, 0)
-    for name in NAMES:
-        message(name).wait_send()
-
-
-def project(student_ref, sum_ref, loss_in_ref, grad_ref, supcon_ref, relation_ref):
-    def one(i, carry):
-        here = pl.ds(pl.multiple_of(i * 16, 16), 16)
         values = student_ref[here, :].astype(F32)
         scaling = lax.rsqrt(jnp.sum(values * values, axis=1, keepdims=True) + epsilon)
         unit = values * scaling
-        grad = sum_ref[here, :]
+        grad = total[there, :] + arrive[0, here, :] + arrive[1, here, :]
         along = jnp.sum(unit * grad, axis=1, keepdims=True)
         grad_ref[here, :] = scaling * (grad - unit * along)
         return carry
 
-    lax.fori_loop(0, student_ref.shape[0] // 16, one, 0)
-    supcon_ref[0, 0] = loss_in_ref[4, 0]
-    relation_ref[0, 0] = loss_in_ref[5, 0]
+    lax.fori_loop(0, rows // 16, finish, 0, unroll=4)
+    for name in NAMES:
+        message(name).wait_send()
+
+
+def deliver(
+    made_hbm, loss_hbm, grad_hbm, supcon_ref, relation_ref, held, loss_ref, load_sem, store_sem
+):
+    rows = held.shape[0]
+    piece = 32
+    loads, stores = [], []
+    for i in range(rows // piece):
+        here = pl.ds(i * piece, piece)
+        loads.append(pltpu.make_async_copy(made_hbm.at[here], held.at[here], load_sem.at[i]))
+        stores.append(pltpu.make_async_copy(held.at[here], grad_hbm.at[here], store_sem.at[i]))
+    loss_load = pltpu.make_async_copy(loss_hbm, loss_ref, load_sem.at[rows // piece])
+    for load in (*loads, loss_load):
+        load.start()
+    for load, store in zip(loads, stores):
+        load.wait()
+        store.start()
+    loss_load.wait()
+    supcon_ref[0, 0] = loss_ref[4, 0]
+    relation_ref[0, 0] = loss_ref[5, 0]
+    for store in stores:
+        store.wait()
 
 
 def body(student, teacher, labels):
@@ -561,7 +573,7 @@
     keys, anchors = 4 * rows, 32 * rows
     vmem = pl.BlockSpec(memory_space=pltpu.VMEM)
     hbm = pl.BlockSpec(memory_space=pltpu.HBM)
-    sums, losses = pl.pallas_call(
+    made, losses = pl.pallas_call(
         kernel,
         out_shape=(
             jax.ShapeDtypeStruct((rows, width), F32),
@@ -607,11 +619,17 @@
     smem = pl.BlockSpec(memory_space=pltpu.SMEM)
     scalar = jax.ShapeDtypeStruct((1, 1), F32)
     grad, supcon, relation = pl.pallas_call(
-        project,
+        deliver,
         out_shape=(jax.ShapeDtypeStruct((rows, width), F32), scalar, scalar),
-        in_specs=[vmem, vmem, smem],
-        out_specs=(vmem, smem, smem),
-    )(student, sums, losses)
+        in_specs=[hbm, hbm],
+        out_specs=(hbm, smem, smem),
+        scratch_shapes=[
+            pltpu.VMEM((rows, width), F32),
+            pltpu.SMEM((8, rows), F32),
+            pltpu.SemaphoreType.DMA((rows // 32 + 1,)),
+            pltpu.SemaphoreType.DMA((rows // 32,)),
+        ],
+    )(made, losses)
     return supcon.reshape(()), relation.reshape(()), grad
 
 

time: 95.1 us -> 94.5 us (level)
    pallas_call x1, Pallas kernels: 3.42 us -> 2.35 us  [body(): pl.pallas_call(deliver, out_shape=(jax.ShapeDtypeStruct((rows, width), F3...]
where the time goes in v6:
time: 94.5 us; the launch traced here: 94.3 us
  Pallas kernels  93.7 us (99%)
    pallas_call x1, Pallas kernels, body(): pl.pallas_call(kernel, out_shape=(jax.ShapeDtypeStruct((rows, width), F32...  91.3 us
    pallas_call x1, Pallas kernels, body(): pl.pallas_call(deliver, out_shape=(jax.ShapeDtypeStruct((rows, width), F3...  2.35 us

profile of v6, /device:TPU:1, one launch (start us, length us, event | category | flops | bytes accessed | tf_op | source)
XLA Modules:
  0.0 94.3 jit_solution(5036393241852537141)
XLA Ops:
  0.6 91.3 %shard_map.58 = (f32[128,1024]{1,0:T(8,128)}, f32[8,128]{1,0:T(8,128)}) custom-call(bf16[128,1024]{1,0:T(8,128)(2,1)} %student_hbm.1, bf16[128,1024]{1,0:T(8,128)(2,1)} %teacher_hbm.1, s32[1,128]{1,0:T(1,128)} %bitcast.3), custom_call_target="tpu_custom_call" | custom-call | tf_op jit(solution)/shard_map/pallas_call | solution.py:576
  92.0 2.4 %shard_map.59 = (f32[128,1024]{1,0:T(8,128)}, f32[1,1]{1,0:T(1,128)}, f32[1,1]{1,0:T(1,128)}) custom-call(f32[128,1024]{1,0:T(8,128)} %get-tuple-element.8.made_hbm, f32[8,128]{1,0:T(8,128)} %get-tuple-element.9.loss_hbm), custom_call_target="tpu_custom_call" | custom-call | tf_op jit(solution)/shard_map/pallas_call | solution.py:621
